TPU v7x, 32 devices: a whole 2x2x4 slice. The times are simulated.
32 devices in a mesh: aa: 2 (over x), ba: 4 (over y, core), col: 4 (over z).
Axes of the slice: x: 2, y: 2, z: 4, core: 2. Of those that a mesh axis runs over, the one named last changes fastest.
Arguments:
- r_rows: bfloat16 [4096, 128], P(('aa', 'ba', 'col')), may hold values from -6 to 6
- r_keys: int32 [4096], P(('aa', 'ba', 'col')), may hold values from 0 to 4095
- r_counts: int32 [256], P(('aa', 'ba', 'col')), may hold values from 0 to 16, as said below
- s_rows: bfloat16 [8192, 128], P(('aa', 'ba', 'col')), may hold values from -6 to 6
- s_keys: int32 [8192], P(('aa', 'ba', 'col')), may hold values from 0 to 4095
- s_counts: int32 [512], P(('aa', 'ba', 'col')), may hold values from 0 to 16, as said below
- t_rows: bfloat16 [4096, 128], P(('aa', 'ba', 'col')), may hold values from -6 to 6
- t_keys: int32 [4096], P(('aa', 'ba', 'col')), may hold values from 0 to 4095
- t_counts: int32 [256], P(('aa', 'ba', 'col')), may hold values from 0 to 16, as said below
Outputs:
- joined: bfloat16 [4096, 128], P(('aa', 'ba', 'col'))
Inputs may be any that keep to these rules, and one draw needn't show every extreme that they name: `r_counts`: in every draw one destination pair, drawn from the seed, gets 16 live slots from every device. `s_counts`: in every draw one destination pair, drawn from the seed, gets 16 live slots from every device. `t_counts`: in every draw one destination pair, drawn from the seed, gets 16 live slots from every device.
All inputs are finite; a program needn't handle non-finite values.
Results may differ from a plain program's by a relative error of at most 0.001.
Values may be sent and summed in bfloat16 or wider, within the bound.
No kernel may reach another device: no remote copies, remote signals or barrier semaphores. Data moves between devices by JAX's collectives and lax.ppermute only.
A program may use at most 64 MiB of HBM per device.

v0:
```python
import jax
import jax.numpy as jnp
from jax import lax
from jax.sharding import PartitionSpec as P

KEYS = 64
CAP = 16


def live_slots(counts):
    place = jnp.arange(CAP, dtype=jnp.int32)
    return (place[None, :] < counts[:, None]).reshape(-1)


def pair_table(keys, rows, live):
    size = KEYS * KEYS
    total = keys.shape[0]
    block = 512
    turns = total // block
    ids = jnp.arange(size, dtype=jnp.int32)

    def add_block(carry, item):
        table, count = carry
        key_block, row_block, live_block = item
        onehot = ((key_block[:, None] == ids[None, :]) & live_block[:, None]).astype(jnp.bfloat16)
        table = table + lax.dot_general(
            onehot, row_block, (((0,), (0,)), ((), ())), preferred_element_type=jnp.float32
        )
        count = count + jnp.sum(onehot, axis=0, dtype=jnp.float32)
        return ((table, count), None)

    start = (jnp.zeros((size, rows.shape[1]), jnp.float32), jnp.zeros((size,), jnp.float32))
    items = (
        keys.reshape(turns, block),
        rows.reshape(turns, block, rows.shape[1]),
        live.reshape(turns, block),
    )
    (table, count), _ = lax.scan(add_block, start, items)
    return (table, count)


def combine(s_table, s_count, t_table, t_count):
    width = s_table.shape[1]
    hi = lax.Precision.HIGHEST
    sd = s_table.reshape(KEYS, KEYS, width)
    scount = s_count.reshape(KEYS, KEYS)
    tu = t_table.reshape(KEYS, KEYS, width)
    tcount = t_count.reshape(KEYS, KEYS)
    total = jnp.einsum("ac,bcw->abw", tcount, sd, precision=hi) + jnp.einsum(
        "bc,acw->abw", scount, tu, precision=hi
    )
    triangles = jnp.einsum("ac,bc->ab", tcount, scount, precision=hi)
    return (total.reshape(KEYS * KEYS, width), triangles.reshape(KEYS * KEYS))


def send_first(rows, keys, counts):
    return (
        lax.all_to_all(rows, ("aa", "ba"), split_axis=0, concat_axis=0, tiled=True),
        lax.all_to_all(keys, ("aa", "ba"), split_axis=0, concat_axis=0, tiled=True),
        lax.all_to_all(counts, ("aa", "ba"), split_axis=0, concat_axis=0, tiled=True),
    )


def send_second(rows, keys, counts):
    return (
        lax.all_to_all(rows, ("ba", "col"), split_axis=0, concat_axis=0, tiled=True),
        lax.all_to_all(keys, ("ba", "col"), split_axis=0, concat_axis=0, tiled=True),
        lax.all_to_all(counts, ("ba", "col"), split_axis=0, concat_axis=0, tiled=True),
    )


def send_third(rows, keys, counts):
    return (
        lax.all_to_all(rows, ("aa", "col"), split_axis=0, concat_axis=0, tiled=True),
        lax.all_to_all(keys, ("aa", "col"), split_axis=0, concat_axis=0, tiled=True),
        lax.all_to_all(counts, ("aa", "col"), split_axis=0, concat_axis=0, tiled=True),
    )


def send_home(joined):
    return lax.all_to_all(joined, ("aa", "ba"), split_axis=0, concat_axis=0, tiled=True)


def body(r_rows, r_keys, r_counts, s_rows, s_keys, s_counts, t_rows, t_keys, t_counts):
    r_held, r_key_held, r_count_held = send_first(r_rows, r_keys, r_counts)
    s_held, s_key_held, s_count_held = send_second(s_rows, s_keys, s_counts)
    t_held, t_key_held, t_count_held = send_third(t_rows, t_keys, t_counts)
    r_live = live_slots(r_count_held)
    r_key_all = lax.all_gather(r_key_held, "col", axis=0, tiled=True)
    s_all, s_key_all, s_count_all = (
        lax.all_gather(s_held, "aa", axis=0, tiled=True),
        lax.all_gather(s_key_held, "aa", axis=0, tiled=True),
        lax.all_gather(s_count_held, "aa", axis=0, tiled=True),
    )
    t_all, t_key_all, t_count_all = (
        lax.all_gather(t_held, "ba", axis=0, tiled=True),
        lax.all_gather(t_key_held, "ba", axis=0, tiled=True),
        lax.all_gather(t_count_held, "ba", axis=0, tiled=True),
    )
    s_table, s_count = pair_table(s_key_all, s_all, live_slots(s_count_all))
    t_table, t_count = pair_table(t_key_all, t_all, live_slots(t_count_all))
    total, triangles = combine(s_table, s_count, t_table, t_count)
    rows_total = jnp.take(total, r_key_all, axis=0)
    rows_count = jnp.take(triangles, r_key_all, axis=0)
    mine, counted = (
        lax.psum_scatter(rows_total, "col", scatter_dimension=0, tiled=True),
        lax.psum_scatter(rows_count, "col", scatter_dimension=0, tiled=True),
    )
    value = r_held.astype(jnp.float32) * mine / jnp.sqrt(1.0 + counted)[:, None]
    joined = jnp.where(r_live[:, None], value, 0.0).astype(jnp.bfloat16)
    return send_home(joined)


def solution(mesh):
    placed = (
        P(("aa", "ba", "col"), None),
        P(("aa", "ba", "col")),
        P(("aa", "ba", "col")),
        P(("aa", "ba", "col"), None),
        P(("aa", "ba", "col")),
        P(("aa", "ba", "col")),
        P(("aa", "ba", "col"), None),
        P(("aa", "ba", "col")),
        P(("aa", "ba", "col")),
    )
    return jax.shard_map(
        body, mesh=mesh, in_specs=placed, out_specs=P(("aa", "ba", "col"), None), check_vma=False
    )
```

profile of v0, /device:TPU:0, one launch (start us, length us, event | category | flops | bytes accessed | tf_op | source)
XLA Modules:
  0.0 162.0 jit_solution(4358317380346819120)
XLA Ops:
  6.5 1.3 copy.32
  7.9 7.3 %all-to-all-start.4 = ((s32[8,1,1]{2,1,0:T(1,128)}), s32[8,1,1]{2,1,0:T(1,128)S(1)}, u32[]{:S(2)}, u32[]{:S(2)}) async-start(s32[8,1,1]{2,1,0:T(1,128)} %copy.32), calls=%async_computation.4 | async-start | bytes 8192 | tf_op jit(solution)/shard_map/all_to_all | solution.py:76
  15.1 1.3 all_to_all.83
  16.5 1.4 all_to_all.89
  19.1 1.3 dynamic-slice.5
  20.3 1.3 copy.34
  21.7 1.3 all_to_all.80
  24.2 6.2 %all-to-all-start.6 = ((s32[16,1,1]{2,1,0:T(1,128)}), s32[16,1,1]{2,1,0:T(1,128)S(1)}, u32[]{:S(2)}, u32[]{:S(2)}) async-start(s32[16,1,1]{2,1,0:T(1,128)} %copy.34), calls=%async_computation.6 | async-start | bytes 16384 | tf_op jit(solution)/shard_map/all_to_all | solution.py:68
  30.9 5.3 %all-reduce = s32[32]{0:T(128)S(1)} all-reduce(s32[32]{0:T(128)S(1)} %dynamic-update-slice), channel_id=2, replica_groups=mesh['aa'=2,'ba'=4,'col'=4] {'ba'}, use_global_device_ids=true, to_apply=%add | all-reduce | flops 32 | bytes 256
  36.8 3.3 %all-to-all-start.2 = ((s32[8,16,1]{1,2,0:T(1,128)}), s32[8,16,1]{1,2,0:T(1,128)S(1)}, u32[]{:S(2)}, u32[]{:S(2)}) async-start(s32[8,16,1]{1,2,0:T(1,128)} %bitcast.3), calls=%async_computation.2 | async-start | bytes 8192 | tf_op jit(solution)/shard_map/all_to_all | solution.py:59
  40.8 4.3 %all-reduce.1 = s32[32]{0:T(128)S(1)} all-reduce(s32[32]{0:T(128)S(1)} %dynamic-update-slice.1), channel_id=3, replica_groups=mesh['aa'=2,'ba'=4,'col'=4] {'aa'}, use_global_device_ids=true, to_apply=%add.1 | all-reduce | flops 32 | bytes 256
  45.2 5.5 %all-to-all-start.3 = ((s32[8,16,1]{1,2,0:T(1,128)}), s32[8,16,1]{1,2,0:T(1,128)S(1)}, u32[]{:S(2)}, u32[]{:S(2)}) async-start(s32[8,16,1]{1,2,0:T(1,128)} %bitcast.5), calls=%async_computation.3 | async-start | bytes 8192 | tf_op jit(solution)/shard_map/all_to_all | solution.py:75
  52.1 11.4 %all-gather.2 = s32[4,1,128]{2,1,0:T(1,128)S(1)} all-gather(s32[1,1,128]{2,1,0:T(1,128)S(1)} %reshape.169), channel_id=1, replica_groups=mesh['aa'=2,'ba'=4,'col'=4] {'col'}, dimensions={0}, use_global_device_ids=true | all-gather | bytes 2560 | tf_op jit(solution)/shard_map/all_gather | solution.py:89
  63.5 3.5 %all-to-all-start.5 = ((s32[16,16,1]{1,2,0:T(1,128)}), s32[16,16,1]{1,2,0:T(1,128)S(1)}, u32[]{:S(2)}, u32[]{:S(2)}) async-start(s32[16,16,1]{1,2,0:T(1,128)} %bitcast.9), calls=%async_computation.5 | async-start | bytes 16384 | tf_op jit(solution)/shard_map/all_to_all | solution.py:67
  67.8 5.1 %all-gather.3 = s32[4,1,128]{2,1,0:T(1,128)S(1)} all-gather(s32[1,1,128]{2,1,0:T(1,128)S(1)} %reshape.171), channel_id=1, replica_groups=mesh['aa'=2,'ba'=4,'col'=4] {'ba'}, dimensions={0}, use_global_device_ids=true | all-gather | bytes 2560 | tf_op jit(solution)/shard_map/all_gather | solution.py:97
  72.8 2.2 %convert_reduce_fusion.1 = f32[4096]{0:T(1024)S(1)} fusion(s32[512]{0:T(512)S(1)} %bitcast.48, pred[512]{0:T(512)(128)(4,1)S(1)} %lt.86), kind=kLoop, calls=%fused_computation.4 | loop fusion | flops 10481664 | bytes 18944 | tf_op jit(solution)/shard_map/while/body/eval_jaxpr/reduce_sum | solution.py:29
  75.2 5.8 %all-to-all-start.8 = ((bf16[8,16,128]{2,1,0:T(8,128)(2,1)}), bf16[8,16,128]{2,1,0:T(8,128)(2,1)S(1)}, u32[]{:S(2)}, u32[]{:S(2)}) async-start(bf16[8,16,128]{2,1,0:T(8,128)(2,1)} %bitcast.45), calls=%async_computation.8 | async-start | bytes 65536 | tf_op jit(solution)/shard_map/all_to_all | solution.py:74
  81.8 4.2 %all-gather.4 = s32[2,1,256]{2,1,0:T(1,128)S(1)} all-gather(s32[1,1,256]{2,1,0:T(1,128)S(1)} %reshape.173), channel_id=1, replica_groups=mesh['aa'=2,'ba'=4,'col'=4] {'aa'}, dimensions={0}, use_global_device_ids=true | all-gather | bytes 3072 | tf_op jit(solution)/shard_map/all_gather | solution.py:92
  86.0 2.2 %convert_reduce_fusion = f32[4096]{0:T(1024)S(1)} fusion(s32[512]{0:T(512)S(1)} %bitcast.50, pred[512]{0:T(512)(128)(4,1)S(1)} %lt.90), kind=kLoop, calls=%fused_computation.2 | loop fusion | flops 10481664 | bytes 18944 | tf_op jit(solution)/shard_map/while/body/eval_jaxpr/reduce_sum | solution.py:29
  88.6 3.1 %gather_fusion.1 = f32[512]{0:T(512)S(1)} fusion(f32[4096]{0:T(1024)S(1)} %reshape.141, s32[1024]{0:T(1024)S(1)} %pad_clamp_fusion), kind=kCustom, calls=%fused_computation.1 | custom fusion | bytes 6144 | tf_op jit(solution)/shard_map/jit(_take)/gather | solution.py:104
  91.8 6.2 %all-to-all-start.7 = ((bf16[16,16,128]{2,1,0:T(8,128)(2,1)}), bf16[16,16,128]{2,1,0:T(8,128)(2,1)S(1)}, u32[]{:S(2)}, u32[]{:S(2)}) async-start(bf16[16,16,128]{2,1,0:T(8,128)(2,1)} %bitcast.13), calls=%async_computation.7 | async-start | bytes 131072 | tf_op jit(solution)/shard_map/all_to_all | solution.py:66
  98.0 5.8 %all_gather.27 = bf16[512,128]{1,0:T(8,128)(2,1)S(1)} all-gather(bf16[128,128]{1,0:T(8,128)(2,1)S(1)} %bitcast.42), channel_id=1, replica_groups=mesh['aa'=2,'ba'=4,'col'=4] {'ba'}, dimensions={0}, use_global_device_ids=true | all-gather | bytes 163840 | tf_op jit(solution)/shard_map/all_gather | solution.py:96
  103.8 1.6 fusion.4
  105.4 2.0 %fusion.22 = f32[64,128,64]{1,2,0:T(8,128)S(1)} fusion(f32[64,64,128]{2,1,0:T(8,128)S(1)} %fusion.4, f32[64,64,1]{1,0,2:T(8,128)S(1)} %reshape.187), kind=kOutput, calls=%fused_computation.40 | convolution fusion | flops 402653184 | bytes 4210688 | tf_op jit(solution)/shard_map/bc,acw->abw/dot_general | solution.py:49
  107.4 5.0 %all_gather.26 = bf16[512,128]{1,0:T(8,128)(2,1)S(1)} all-gather(bf16[256,128]{1,0:T(8,128)(2,1)S(1)} %bitcast.41), channel_id=1, replica_groups=mesh['aa'=2,'ba'=4,'col'=4] {'aa'}, dimensions={0}, use_global_device_ids=true | all-gather | bytes 196608 | tf_op jit(solution)/shard_map/all_gather | solution.py:91
  112.4 1.6 fusion.7
  114.1 3.1 %bitcast_add_fusion = f32[64,64,128]{2,0,1:T(8,128)S(1)} fusion(f32[64,128,64]{1,2,0:T(8,128)S(1)} %fusion.22, f32[64,64,1]{1,0,2:T(8,128)S(1)} %reshape.185, f32[64,64,128]{2,1,0:T(8,128)S(1)} %fusion.7), kind=kOutput, calls=%fused_computation.22 | convolution fusion | flops 403177472 | bytes 6307840 | tf_op jit(solution)/shard_map/ac,bcw->abw/dot_general | solution.py:49
  121.0 4.0 %all-to-all-start = ((s32[8,1,1]{2,1,0:T(1,128)}), s32[8,1,1]{2,1,0:T(1,128)S(1)}, u32[]{:S(2)}, u32[]{:S(2)}) async-start(s32[8,1,1]{2,1,0:T(1,128)} %copy.29), calls=%async_computation | async-start | bytes 8192 | tf_op jit(solution)/shard_map/all_to_all | solution.py:60
  126.3 3.2 %all-to-all-done = s32[8,1,1]{2,1,0:T(1,128)S(1)} async-done(((s32[8,1,1]{2,1,0:T(1,128)}), s32[8,1,1]{2,1,0:T(1,128)S(1)}, u32[]{:S(2)}, u32[]{:S(2)}) %all-to-all-start) | async-done | bytes 64 | tf_op jit(solution)/shard_map/all_to_all | solution.py:60
  129.6 3.3 %all-to-all-start.1 = ((bf16[8,16,128]{2,1,0:T(8,128)(2,1)}), bf16[8,16,128]{2,1,0:T(8,128)(2,1)S(1)}, u32[]{:S(2)}, u32[]{:S(2)}) async-start(bf16[8,16,128]{2,1,0:T(8,128)(2,1)} %bitcast.1), calls=%async_computation.1 | async-start | bytes 65536 | tf_op jit(solution)/shard_map/all_to_all | solution.py:58
  133.3 11.5 %all-reduce.2 = f32[512]{0:T(512)S(1)} all-reduce(f32[512]{0:T(512)S(1)} %get-tuple-element.31), channel_id=5, replica_groups=mesh['aa'=2,'ba'=4,'col'=4] {'col'}, use_global_device_ids=true, to_apply=%region_3.4.clone | all-reduce | flops 512 | bytes 4096
  145.9 8.7 %all_to_all.114 = bf16[8,16,128]{2,1,0:T(8,128)(2,1)S(1)} all-to-all(bf16[8,16,128]{2,1,0:T(8,128)(2,1)S(1)} %bitcast.44), channel_id=1, replica_groups=mesh['aa'=2,'ba'=4,'col'=4] {'aa','ba'}, dimensions={0} | all-to-all | bytes 65536 | tf_op jit(solution)/shard_map/all_to_all | solution.py:81
  (54 shorter events, 13.2 us)
Async XLA Ops:
  7.9 16.4 %all-to-all-start.4 = ((s32[8,1,1]{2,1,0:T(1,128)}), s32[8,1,1]{2,1,0:T(1,128)S(1)}, u32[]{:S(2)}, u32[]{:S(2)}) async-start(s32[8,1,1]{2,1,0:T(1,128)} %copy.32), calls=%async_computation.4 | async-start | bytes 8192 | tf_op jit(solution)/shard_map/all_to_all | solution.py:76
  24.2 12.6 %all-to-all-start.6 = ((s32[16,1,1]{2,1,0:T(1,128)}), s32[16,1,1]{2,1,0:T(1,128)S(1)}, u32[]{:S(2)}, u32[]{:S(2)}) async-start(s32[16,1,1]{2,1,0:T(1,128)} %copy.34), calls=%async_computation.6 | async-start | bytes 16384 | tf_op jit(solution)/shard_map/all_to_all | solution.py:68
  36.8 8.4 %all-to-all-start.2 = ((s32[8,16,1]{1,2,0:T(1,128)}), s32[8,16,1]{1,2,0:T(1,128)S(1)}, u32[]{:S(2)}, u32[]{:S(2)}) async-start(s32[8,16,1]{1,2,0:T(1,128)} %bitcast.3), calls=%async_computation.2 | async-start | bytes 8192 | tf_op jit(solution)/shard_map/all_to_all | solution.py:59
  45.2 18.3 %all-to-all-start.3 = ((s32[8,16,1]{1,2,0:T(1,128)}), s32[8,16,1]{1,2,0:T(1,128)S(1)}, u32[]{:S(2)}, u32[]{:S(2)}) async-start(s32[8,16,1]{1,2,0:T(1,128)} %bitcast.5), calls=%async_computation.3 | async-start | bytes 8192 | tf_op jit(solution)/shard_map/all_to_all | solution.py:75
  63.5 11.7 %all-to-all-start.5 = ((s32[16,16,1]{1,2,0:T(1,128)}), s32[16,16,1]{1,2,0:T(1,128)S(1)}, u32[]{:S(2)}, u32[]{:S(2)}) async-start(s32[16,16,1]{1,2,0:T(1,128)} %bitcast.9), calls=%async_computation.5 | async-start | bytes 16384 | tf_op jit(solution)/shard_map/all_to_all | solution.py:67
  75.2 16.6 %all-to-all-start.8 = ((bf16[8,16,128]{2,1,0:T(8,128)(2,1)}), bf16[8,16,128]{2,1,0:T(8,128)(2,1)S(1)}, u32[]{:S(2)}, u32[]{:S(2)}) async-start(bf16[8,16,128]{2,1,0:T(8,128)(2,1)} %bitcast.45), calls=%async_computation.8 | async-start | bytes 65536 | tf_op jit(solution)/shard_map/all_to_all | solution.py:74
  91.8 15.6 %all-to-all-start.7 = ((bf16[16,16,128]{2,1,0:T(8,128)(2,1)}), bf16[16,16,128]{2,1,0:T(8,128)(2,1)S(1)}, u32[]{:S(2)}, u32[]{:S(2)}) async-start(bf16[16,16,128]{2,1,0:T(8,128)(2,1)} %bitcast.13), calls=%async_computation.7 | async-start | bytes 131072 | tf_op jit(solution)/shard_map/all_to_all | solution.py:66
  98.0 47.0 %reduce-scatter.2.cloned.1.call-start = ((), (), s32[]{:S(2)}) async-start(), calls=%async_computation.11 | async-start | bytes 327680 | tf_op jit(solution)/shard_map/reduce_scatter | solution.py:106
  118.3 1.9 %copy-start = (s32[8]{0:T(128)S(1)}, s32[8]{0:T(128)}, u32[]{:S(2)}) copy-start(s32[8]{0:T(128)} %param.11) | copy-start | bytes 100
  118.4 6.6 %copy-start.1 = (u32[32]{0:T(128)S(1)}, u32[32]{0:T(128)}, u32[]{:S(2)}) copy-start(u32[32]{0:T(128)} %constant.76) | copy-start | bytes 388
  121.0 8.6 %all-to-all-start = ((s32[8,1,1]{2,1,0:T(1,128)}), s32[8,1,1]{2,1,0:T(1,128)S(1)}, u32[]{:S(2)}, u32[]{:S(2)}) async-start(s32[8,1,1]{2,1,0:T(1,128)} %copy.29), calls=%async_computation | async-start | bytes 8192 | tf_op jit(solution)/shard_map/all_to_all | solution.py:60
  129.6 15.4 %all-to-all-start.1 = ((bf16[8,16,128]{2,1,0:T(8,128)(2,1)}), bf16[8,16,128]{2,1,0:T(8,128)(2,1)S(1)}, u32[]{:S(2)}, u32[]{:S(2)}) async-start(bf16[8,16,128]{2,1,0:T(8,128)(2,1)} %bitcast.1), calls=%async_computation.1 | async-start | bytes 65536 | tf_op jit(solution)/shard_map/all_to_all | solution.py:58
Sparse Core Ops, SparseCore 0:
  120.4 21.0 reduce-scatter.1
where the time goes:
time: 163 us; the launch traced here: 162 us
  blocking collectives  61.2 us (38%)
  starting transfers between devices  45.1 us (28%)
  local copies, waits for them, and re-layouts  18.5 us (11%)
  between operations  15.6 us (10%)
  other arithmetic  9.47 us (6%)
  matrix products  8.48 us (5%)
  waiting for transfers between devices  3.68 us (2%)
    unnamed x3, blocking collectives  21.1 us
    all_gather x1, blocking collectives, body(): r_key_all = lax.all_gather(r_key_held, 'col', axis=0, tiled=True)  11.4 us
    all_to_all x1, blocking collectives, send_home(): lax.all_to_all(joined, ('aa', 'ba'), split_axis=0, concat_axis=0, tiled=T...  8.68 us
    all_to_all x1, starting transfers between devices, send_third(): lax.all_to_all(counts, ('aa', 'col'), split_axis=0, concat_axis=0, tiled=...  7.28 us
    all_to_all x1, starting transfers between devices, send_second(): lax.all_to_all(counts, ('ba', 'col'), split_axis=0, concat_axis=0, tiled=...  6.17 us
    all_to_all x1, starting transfers between devices, send_second(): lax.all_to_all(rows, ('ba', 'col'), split_axis=0, concat_axis=0, tiled=True)  6.16 us
    all_to_all x1, starting transfers between devices, send_third(): lax.all_to_all(rows, ('aa', 'col'), split_axis=0, concat_axis=0, tiled=True)  5.8 us
    all_gather x1, blocking collectives, body(): lax.all_gather(t_held, 'ba', axis=0, tiled=True)  5.78 us
  transfers between devices with their start and end apart: 10, of which 2 were waited for; matrix products, arithmetic and copies ran while one was open for 13% of the time, Pallas kernels for 0%

commit v1 on v0

v1 whole, which is shorter than its diff:
```python
import functools

import jax
import jax.numpy as jnp
from jax import lax
from jax.experimental import pallas as pl
from jax.experimental.pallas import tpu as pltpu
from jax.sharding import PartitionSpec as P

KEYS = 64
LANES = 128
META = 8
AXES = ("aa", "ba", "col")
f32 = jnp.float32
bf16 = jnp.bfloat16


def iota(shape, dim):
    return lax.broadcasted_iota(jnp.int32, shape, dim)


def split(x):
    hi = x.astype(bf16)
    return hi, (x - hi.astype(f32)).astype(bf16)


def mm(x, y):
    return lax.dot_general(x, y, (((1,), (0,)), ((), ())), preferred_element_type=f32)


def mm_nt(x, y):
    return lax.dot_general(x, y, (((1,), (1,)), ((), ())), preferred_element_type=f32)


def mm_tn(x, y):
    return lax.dot_general(x, y, (((0,), (0,)), ((), ())), preferred_element_type=f32)


def pack_kernel(
    n_a, n_b, n_c, cap, s_rows, t_rows, s_keys, t_keys, r_keys, s_cnt, t_cnt, r_cnt, out
):
    def halves(keys_ref, cnt_ref):
        keys = keys_ref[...]
        slots = keys.shape[1]
        groups = slots // cap
        spread = (iota((groups, slots), 1) // cap == iota((groups, slots), 0)).astype(bf16)
        cnt = jnp.broadcast_to(cnt_ref[...].astype(f32).astype(bf16), (8, groups))
        live = (iota((1, slots), 1) % cap).astype(f32) < mm(cnt, spread)[0:1]
        first = jnp.where(live, (keys // KEYS).astype(f32), -1.0)
        second = jnp.where(live, (keys % KEYS).astype(f32), -1.0)
        return first, second

    def at(vec, start):
        row = vec[:, start // LANES * LANES : (start // LANES + 1) * LANES]
        return pltpu.roll(row, (LANES - start % LANES) % LANES, 1) if start % LANES else row

    sb, sc = halves(s_keys, s_cnt)
    ta, tc = halves(t_keys, t_cnt)
    ra, rb = halves(r_keys, r_cnt)
    seg = n_c * cap
    row = iota((META, LANES), 0)
    for a in range(n_a):
        for b in range(n_b):
            rows = (
                at(sb, b * seg),
                at(sc, b * seg),
                at(ta, a * seg),
                at(tc, a * seg),
                at(ra, (a * n_b + b) * cap),
                at(rb, (a * n_b + b) * cap),
            )
            meta = jnp.zeros((META, LANES), f32)
            for k, value in enumerate(rows):
                meta = jnp.where(row == k, value, meta)
            meta = meta.astype(bf16)
            for c in range(n_c):
                d = (a * n_b + b) * n_c + c
                g, h = b * n_c + c, a * n_c + c
                out[d, 0:cap, :] = s_rows[g * cap : (g + 1) * cap, :]
                out[d, cap : 2 * cap, :] = t_rows[h * cap : (h + 1) * cap, :]
                out[d, 2 * cap : 2 * cap + META, :] = meta


def join_kernel(n_c, cap, srcs, held, out, sb_ref, sc_ref, ta_ref, tc_ref, pq_ref, f_ref):
    blocks = held.shape[0] // srcs
    m = srcs * cap
    wide = n_c * KEYS
    own = lax.axis_index("col")
    place = iota((cap, LANES), 1) % cap == iota((cap, LANES), 0)
    lane_c = iota((LANES, wide), 0) // cap
    sel_all = (lane_c == iota((LANES, wide), 1) // KEYS).astype(bf16)
    sel_first = (lane_c == 0).astype(bf16)
    here = iota((m, wide), 1) // KEYS == own
    key_all = (iota((m, wide), 1) % KEYS).astype(f32)

    def onehot(meta, kind, sel):
        rep = jnp.broadcast_to(meta[:, kind : kind + 1, :], (srcs, cap, LANES))
        rep = jnp.where(place[None], rep, 0.0).astype(bf16).reshape(m, LANES)
        return mm(rep, sel) == key_all

    def tables(i):
        meta = held[pl.ds(i * srcs, srcs), 2 * cap : 2 * cap + META, :].astype(f32)
        at = pl.ds(i * m, m)
        sb = onehot(meta, 0, sel_all)
        sc = onehot(meta, 1, sel_all)
        ta = onehot(meta, 2, sel_all)
        tc = onehot(meta, 3, sel_all)
        f_ref[0] += mm_tn(sb.astype(bf16), sc.astype(bf16))
        f_ref[1] += mm_tn(ta.astype(bf16), tc.astype(bf16))
        sb_ref[at] = (sb & here).astype(bf16)
        sc_ref[at] = (sc & here).astype(bf16)
        ta_ref[at] = (ta & here).astype(bf16)
        tc_ref[at] = (tc & here).astype(bf16)

    def joins(i):
        meta = held[pl.ds(i * srcs, srcs), 2 * cap : 2 * cap + META, :].astype(f32)
        ra = onehot(meta, 4, sel_first).astype(bf16)
        rb = onehot(meta, 5, sel_first).astype(bf16)
        xa = mm(ra, pq_ref[2]) + mm(ra, pq_ref[3])
        xb = mm(rb, pq_ref[0]) + mm(rb, pq_ref[1])
        triangles = jnp.sum(xa * xb, axis=1, keepdims=True)
        scale = 1.0 / jnp.sqrt(1.0 + triangles)
        xa_hi, xa_lo = split(xa)
        xb_hi, xb_lo = split(xb)

        def one(j, acc):
            at = pl.ds(j * m, m)
            sb, sc, ta, tc = sb_ref[at], sc_ref[at], ta_ref[at], tc_ref[at]
            rows = held[pl.ds(j * srcs, srcs), 0 : 2 * cap, :]
            s = rows[:, 0:cap, :].reshape(m, LANES)
            t = rows[:, cap : 2 * cap, :].reshape(m, LANES)
            hi, lo = split((mm_nt(xa_hi, sc) + mm_nt(xa_lo, sc)) * mm_nt(rb, sb))
            acc = acc + mm(hi, s) + mm(lo, s)
            hi, lo = split((mm_nt(xb_hi, tc) + mm_nt(xb_lo, tc)) * mm_nt(ra, ta))
            return acc + mm(hi, t) + mm(lo, t)

        acc = jnp.zeros((m, LANES), f32)
        acc = one(0, acc) if blocks == 1 else lax.fori_loop(0, blocks, one, acc)
        out[pl.ds(i * srcs, srcs)] = (acc * scale).reshape(srcs, cap, LANES)

    def each(step):
        if blocks == 1:
            step(0)
        else:
            pl.loop(0, blocks)(step)

    f_ref[...] = jnp.zeros_like(f_ref)
    each(tables)
    same = iota((wide, wide), 0) // KEYS == iota((wide, wide), 1) // KEYS
    for k in range(2):
        hi, lo = split(jnp.where(same, f_ref[k], 0.0))
        pq_ref[2 * k] = hi
        pq_ref[2 * k + 1] = lo
    each(joins)


def body(sizes, r_rows, r_keys, r_counts, s_rows, s_keys, s_counts, t_rows, t_keys, t_counts):
    n_a, n_b, n_c = sizes
    n = n_a * n_b * n_c
    cap = r_keys.shape[0] // r_counts.shape[0]
    width = r_rows.shape[1]
    srcs = max(512 // cap, 1)
    srcs = srcs if n % srcs == 0 else n
    total_slots = n * cap
    wide = n_c * KEYS
    row = lambda x: x.reshape(1, x.shape[0])
    packed = pl.pallas_call(
        functools.partial(pack_kernel, n_a, n_b, n_c, cap),
        out_shape=jax.ShapeDtypeStruct((n, 2 * cap + META, width), bf16),
        name="pack",
    )(
        s_rows, t_rows, row(s_keys), row(t_keys), row(r_keys),
        row(s_counts), row(t_counts), row(r_counts),
    )
    held = lax.all_to_all(packed, AXES, split_axis=0, concat_axis=0, tiled=True)
    shares = pl.pallas_call(
        functools.partial(join_kernel, n_c, cap, srcs),
        out_shape=jax.ShapeDtypeStruct((n, cap, width), f32),
        scratch_shapes=[pltpu.VMEM((total_slots, wide), bf16) for _ in range(4)]
        + [pltpu.VMEM((4, wide, wide), bf16), pltpu.VMEM((2, wide, wide), f32)],
        name="join",
    )(held)
    back = lax.all_to_all(shares, AXES, split_axis=0, concat_axis=0, tiled=True)
    total = jnp.sum(back.reshape(n_a * n_b, n_c, cap, width), axis=1)
    return (r_rows.astype(f32) * total.reshape(r_rows.shape)).astype(bf16)


def solution(mesh):
    rows, flat = P(AXES, None), P(AXES)
    sizes = tuple(mesh.shape[name] for name in AXES)
    return jax.shard_map(
        functools.partial(body, sizes),
        mesh=mesh,
        in_specs=(rows, flat, flat) * 3,
        out_specs=rows,
        check_vma=False,
    )
```

time: 163 us -> 40.1 us (0.25)
  starting transfers between devices: 45.1 us -> 0 us
  blocking collectives: 61.2 us -> 32 us
  local copies, waits for them, and re-layouts: 18.5 us -> 0.74 us
  between operations: 15.6 us -> 0.01 us
  other arithmetic: 9.47 us -> 0.64 us
  matrix products: 8.48 us -> 0 us
  Pallas kernels: 0 us -> 6.31 us
  waiting for transfers between devices: 3.68 us -> 0 us
    all_to_all x9 -> x0, starting transfers between devices: 45.1 us -> none  [the longest x1 7.28 us: send_third(): lax.all_to_all(counts, ('aa', 'col'), split_axis=0, concat_axis=0, tiled=...]
    all_gather x5 -> x0, blocking collectives: 31.4 us -> none  [the longest x1 11.4 us: body(): r_key_all = lax.all_gather(r_key_held, 'col', axis=0, tiled=True)]
    all_to_all x1 -> x2, blocking collectives: 8.68 us -> 32 us  [the longest x1 18.5 us: body(): held = lax.all_to_all(packed, AXES, split_axis=0, concat_axis=0, tiled=True)]
    unnamed x3 -> x0, blocking collectives: 21.1 us -> none
    dot_general x5 -> x0, matrix products: 8.48 us -> none  [the longest x2 3.23 us: add_block(): lax.dot_general(onehot, row_block, (((0,), (0,)), ((), ())), preferred_el...]
    all_to_all x7 -> x0, local copies, waits for them, and re-layouts: 7.91 us -> none  [the longest x2 1.91 us: send_third(): lax.all_to_all(keys, ('aa', 'col'), split_axis=0, concat_axis=0, tiled=True)]
    pallas_call x0 -> x2, Pallas kernels: none -> 6.31 us  [the longest x1 4.47 us: body(): pl.pallas_call(functools.partial(join_kernel, n_c, cap, srcs), out_shape=...]
    reduce_sum x2 -> x1, other arithmetic: 4.39 us -> 0.02 us  [body(): total = jnp.sum(back.reshape(n_a * n_b, n_c, cap, width), axis=1)]
  transfers between devices with their start and end apart: 10 -> 0, of which waited for: 2 -> 0; matrix products, arithmetic and copies ran while one was open for 13% -> 0% of each run, Pallas kernels for 0% -> 0%
where the time goes in v1:
time: 40.1 us; the launch traced here: 39.7 us
  blocking collectives  32 us (80%)
  Pallas kernels  6.31 us (16%)
  local copies, waits for them, and re-layouts  0.74 us (2%)
  other arithmetic  0.64 us (2%)
    all_to_all x1, blocking collectives, body(): held = lax.all_to_all(packed, AXES, split_axis=0, concat_axis=0, tiled=True)  18.5 us
    all_to_all x1, blocking collectives, body(): back = lax.all_to_all(shares, AXES, split_axis=0, concat_axis=0, tiled=True)  13.5 us
    pallas_call x1, Pallas kernels, body(): pl.pallas_call(functools.partial(join_kernel, n_c, cap, srcs), out_shape=...  4.47 us
    pallas_call x1, Pallas kernels, body(): pl.pallas_call(functools.partial(pack_kernel, n_a, n_b, n_c, cap), out_sh...  1.84 us

profile of v1, /device:TPU:0, one launch (start us, length us, event | category | flops | bytes accessed | tf_op | source)
XLA Modules:
  0.0 39.7 jit_solution(17182591316178084969)
XLA Ops:
  0.0 1.8 %pack.1 = bf16[32,40,128]{2,1,0:T(8,128)(2,1)} custom-call(bf16[256,128]{1,0:T(8,128)(2,1)} %s_rows.1, bf16[128,128]{1,0:T(8,128)(2,1)} %t_rows.1, s32[1,256]{1,0:T(1,128)} %bitcast.12, s32[1,128]{1,0:T(1,128)} %bitcast.13, s32[1,128]{1,0:T(1,128)} %bitcast.14, s32[1,16]{1,0:T(1,128)} %bitcast.15, s32[1,8]{1,0:T(1,128)} %bitcast.16, s32[1,8]{1,0:T(1,128)} %bitcast.17), custom_call_target="tpu_custom_call" | custom-call | tf_op jit(solution)/shard_map/pack/pallas_call | solution.py:167
  1.8 18.5 %all_to_all.10.held = bf16[32,40,128]{2,1,0:T(8,128)(2,1)} all-to-all(bf16[32,40,128]{2,1,0:T(8,128)(2,1)} %pack.1), channel_id=1, replica_groups=mesh['aa'=2,'ba'=4,'col'=4] {'aa','ba','col'}, dimensions={0} | all-to-all | bytes 655360 | tf_op jit(solution)/shard_map/all_to_all | solution.py:175
  20.3 4.5 %join.1 = f32[32,16,128]{2,1,0:T(8,128)} custom-call(bf16[32,40,128]{2,1,0:T(8,128)(2,1)} %all_to_all.10.held), custom_call_target="tpu_custom_call" | custom-call | tf_op jit(solution)/shard_map/join/pallas_call | solution.py:176
  24.8 13.5 %all_to_all.11 = f32[32,16,128]{2,1,0:T(8,128)S(1)} all-to-all(f32[32,16,128]{2,1,0:T(8,128)} %join.1), channel_id=1, replica_groups=mesh['aa'=2,'ba'=4,'col'=4] {'aa','ba','col'}, dimensions={0} | all-to-all | bytes 524288 | tf_op jit(solution)/shard_map/all_to_all | solution.py:183
  38.3 0.0 copy-start
  38.3 0.7 %copy-done = bf16[128,128]{1,0:T(8,128)(2,1)S(1)} copy-done((bf16[128,128]{1,0:T(8,128)(2,1)S(1)}, bf16[128,128]{1,0:T(8,128)(2,1)}, u32[]{:S(2)}) %copy-start) | copy-done | bytes 32792
  39.1 0.6 %fusion = bf16[128,128]{1,0:T(8,128)(2,1)} fusion(f32[8,16,128]{2,1,0:T(8,128)S(1)} %bitcast_reduce_fusion, bf16[128,128]{1,0:T(8,128)(2,1)S(1)} %copy-done), kind=kLoop, calls=%fused_computation.2 | loop fusion | flops 49152 | bytes 131072 | tf_op jit(solution)/shard_map/convert_element_type | solution.py:185
  (1 shorter events, 0.0 us)
Async XLA Ops:
  38.3 0.8 %copy-start = (bf16[128,128]{1,0:T(8,128)(2,1)S(1)}, bf16[128,128]{1,0:T(8,128)(2,1)}, u32[]{:S(2)}) copy-start(bf16[128,128]{1,0:T(8,128)(2,1)} %param.9) | copy-start | bytes 98308

commit v2 on v1

--- a/solution.py
+++ b/solution.py
@@ -37,7 +37,7 @@
 
 
 def pack_kernel(
-    n_a, n_b, n_c, cap, s_rows, t_rows, s_keys, t_keys, r_keys, s_cnt, t_cnt, r_cnt, out
+    n_a, n_b, n_c, cap, s_rows, t_rows, s_keys, t_keys, r_keys, s_cnt, t_cnt, r_cnt, r_rows, out, r_out
 ):
     def halves(keys_ref, cnt_ref):
         keys = keys_ref[...]
@@ -54,6 +54,7 @@
         row = vec[:, start // LANES * LANES : (start // LANES + 1) * LANES]
         return pltpu.roll(row, (LANES - start % LANES) % LANES, 1) if start % LANES else row
 
+    r_out[...] = r_rows[...]
     sb, sc = halves(s_keys, s_cnt)
     ta, tc = halves(t_keys, t_cnt)
     ra, rb = halves(r_keys, r_cnt)
@@ -81,6 +82,14 @@
                 out[d, 2 * cap : 2 * cap + META, :] = meta
 
 
+def home_kernel(shares, r_rows, out):
+    groups, n_c, cap, width = shares.shape
+    total = shares[:, 0]
+    for c in range(1, n_c):
+        total = total + shares[:, c]
+    out[...] = (r_rows[...].astype(f32) * total.reshape(out.shape)).astype(bf16)
+
+
 def join_kernel(n_c, cap, srcs, held, out, sb_ref, sc_ref, ta_ref, tc_ref, pq_ref, f_ref):
     blocks = held.shape[0] // srcs
     m = srcs * cap
@@ -164,25 +173,33 @@
     total_slots = n * cap
     wide = n_c * KEYS
     row = lambda x: x.reshape(1, x.shape[0])
-    packed = pl.pallas_call(
+    near = lambda x: pltpu.with_memory_space_constraint(x, pltpu.VMEM)
+    params = pltpu.CompilerParams(vmem_limit_bytes=40 << 20)
+    packed, r_kept = pl.pallas_call(
         functools.partial(pack_kernel, n_a, n_b, n_c, cap),
-        out_shape=jax.ShapeDtypeStruct((n, 2 * cap + META, width), bf16),
+        out_shape=(pltpu.VMEM((n, 2 * cap + META, width), bf16), pltpu.VMEM(r_rows.shape, bf16)),
+        compiler_params=params,
         name="pack",
     )(
         s_rows, t_rows, row(s_keys), row(t_keys), row(r_keys),
-        row(s_counts), row(t_counts), row(r_counts),
+        row(s_counts), row(t_counts), row(r_counts), r_rows,
     )
     held = lax.all_to_all(packed, AXES, split_axis=0, concat_axis=0, tiled=True)
     shares = pl.pallas_call(
         functools.partial(join_kernel, n_c, cap, srcs),
-        out_shape=jax.ShapeDtypeStruct((n, cap, width), f32),
+        out_shape=pltpu.VMEM((n, cap, width), f32),
         scratch_shapes=[pltpu.VMEM((total_slots, wide), bf16) for _ in range(4)]
         + [pltpu.VMEM((4, wide, wide), bf16), pltpu.VMEM((2, wide, wide), f32)],
+        compiler_params=params,
         name="join",
-    )(held)
+    )(near(held))
     back = lax.all_to_all(shares, AXES, split_axis=0, concat_axis=0, tiled=True)
-    total = jnp.sum(back.reshape(n_a * n_b, n_c, cap, width), axis=1)
-    return (r_rows.astype(f32) * total.reshape(r_rows.shape)).astype(bf16)
+    return pl.pallas_call(
+        home_kernel,
+        out_shape=jax.ShapeDtypeStruct(r_rows.shape, bf16),
+        compiler_params=params,
+        name="home",
+    )(near(back.reshape(n_a * n_b, n_c, cap, width)), near(r_kept))
 
 
 def solution(mesh):

time: 40.1 us -> 38.6 us (0.963)
  Pallas kernels: 6.31 us -> 3.65 us
  local copies, waits for them, and re-layouts: 0.74 us -> 3.08 us
  other arithmetic: 0.64 us -> 0 us
  blocking collectives: 32 us -> 31.5 us
    unnamed x2 -> x18, local copies, waits for them, and re-layouts: 0.74 us -> 3.08 us
    pallas_call x1, Pallas kernels: 4.47 us -> 2.8 us  [body(): pl.pallas_call(functools.partial(join_kernel, n_c, cap, srcs), out_shape=...]
    pallas_call x1, Pallas kernels: 1.84 us -> 0.21 us  [body(): pl.pallas_call(functools.partial(pack_kernel, n_a, n_b, n_c, cap), out_sh...]
    pallas_call x0 -> x1, Pallas kernels: none -> 0.64 us  [body(): pl.pallas_call(home_kernel, out_shape=jax.ShapeDtypeStruct(r_rows.shape,...]
    convert_element_type x1 -> x0, other arithmetic: 0.62 us -> none  [body(): return (r_rows.astype(f32) * total.reshape(r_rows.shape)).astype(bf16)]
where the time goes in v2:
time: 38.6 us; the launch traced here: 38.2 us
  blocking collectives  31.5 us (82%)
  Pallas kernels  3.65 us (9%)
  local copies, waits for them, and re-layouts  3.08 us (8%)
    all_to_all x1, blocking collectives, body(): held = lax.all_to_all(packed, AXES, split_axis=0, concat_axis=0, tiled=True)  18.2 us
    all_to_all x1, blocking collectives, body(): back = lax.all_to_all(shares, AXES, split_axis=0, concat_axis=0, tiled=True)  13.3 us
    unnamed x18, local copies, waits for them, and re-layouts  3.08 us
    pallas_call x1, Pallas kernels, body(): pl.pallas_call(functools.partial(join_kernel, n_c, cap, srcs), out_shape=...  2.8 us

profile of v2, /device:TPU:0, one launch (start us, length us, event | category | flops | bytes accessed | tf_op | source)
XLA Modules:
  0.0 38.2 jit_solution(17048074808477722623)
XLA Ops:
  0.0 0.0 copy-start.5
  0.0 0.0 copy-start.6
  0.0 0.0 copy-start.7
  0.0 0.0 copy-start.8
  0.0 0.0 copy-start.3
  0.0 0.0 copy-start.4
  0.0 0.6 %copy-done.5 = s32[128]{0:T(128)S(1)} copy-done((s32[128]{0:T(128)S(1)}, s32[128]{0:T(128)}, u32[]{:S(2)}) %copy-start.5) | copy-done | bytes 536
  0.7 0.0 copy-done.6
  0.7 0.0 copy-done.7
  0.7 0.0 copy-done.8
  0.7 0.0 copy-done.3
  0.7 0.0 copy-done.4
  0.7 0.0 copy-start
  0.7 0.8 %copy-done = bf16[256,128]{1,0:T(8,128)(2,1)S(1)} copy-done((bf16[256,128]{1,0:T(8,128)(2,1)S(1)}, bf16[256,128]{1,0:T(8,128)(2,1)}, u32[]{:S(2)}) %copy-start) | copy-done | bytes 65560
  1.6 0.0 copy-start.1
  1.6 0.8 %copy-done.1 = bf16[128,128]{1,0:T(8,128)(2,1)S(1)} copy-done((bf16[128,128]{1,0:T(8,128)(2,1)S(1)}, bf16[128,128]{1,0:T(8,128)(2,1)}, u32[]{:S(2)}) %copy-start.1) | copy-done | bytes 32792
  2.3 0.0 copy-start.2
  2.3 0.8 %copy-done.2 = bf16[128,128]{1,0:T(8,128)(2,1)S(1)} copy-done((bf16[128,128]{1,0:T(8,128)(2,1)S(1)}, bf16[128,128]{1,0:T(8,128)(2,1)}, u32[]{:S(2)}) %copy-start.2) | copy-done | bytes 32792
  3.1 0.2 pack.1
  3.3 18.2 %all_to_all.10.held = bf16[32,40,128]{2,1,0:T(8,128)(2,1)S(1)} all-to-all(bf16[32,40,128]{2,1,0:T(8,128)(2,1)S(1)} %get-tuple-element.7), channel_id=1, replica_groups=mesh['aa'=2,'ba'=4,'col'=4] {'aa','ba','col'}, dimensions={0} | all-to-all | bytes 655360 | tf_op jit(solution)/shard_map/all_to_all | solution.py:187
  21.5 2.8 %join.1 = f32[32,16,128]{2,1,0:T(8,128)S(1)} custom-call(bf16[32,40,128]{2,1,0:T(8,128)(2,1)S(1)} %all_to_all.10.held), custom_call_target="tpu_custom_call" | custom-call | tf_op jit(solution)/shard_map/join/pallas_call | solution.py:188
  24.3 13.3 %all_to_all.11 = f32[32,16,128]{2,1,0:T(8,128)S(1)} all-to-all(f32[32,16,128]{2,1,0:T(8,128)S(1)} %join.1), channel_id=1, replica_groups=mesh['aa'=2,'ba'=4,'col'=4] {'aa','ba','col'}, dimensions={0} | all-to-all | bytes 524288 | tf_op jit(solution)/shard_map/all_to_all | solution.py:196
  37.6 0.6 %home.1 = bf16[128,128]{1,0:T(8,128)(2,1)} custom-call(f32[8,4,16,128]{3,2,1,0:T(8,128)S(1)} %bitcast.7, bf16[128,128]{1,0:T(8,128)(2,1)S(1)} %get-tuple-element.8.r_rows), custom_call_target="tpu_custom_call" | custom-call | tf_op jit(solution)/shard_map/home/pallas_call | solution.py:197
Async XLA Ops:
  0.0 0.7 %copy-start.5 = (s32[128]{0:T(128)S(1)}, s32[128]{0:T(128)}, u32[]{:S(2)}) copy-start(s32[128]{0:T(128)} %param.10) | copy-start | bytes 1540
  0.0 0.7 %copy-start.6 = (s32[16]{0:T(128)S(1)}, s32[16]{0:T(128)}, u32[]{:S(2)}) copy-start(s32[16]{0:T(128)} %param.14) | copy-start | bytes 196
  0.0 0.7 %copy-start.7 = (s32[8]{0:T(128)S(1)}, s32[8]{0:T(128)}, u32[]{:S(2)}) copy-start(s32[8]{0:T(128)} %param.17) | copy-start | bytes 100
  0.0 0.7 %copy-start.8 = (s32[8]{0:T(128)S(1)}, s32[8]{0:T(128)}, u32[]{:S(2)}) copy-start(s32[8]{0:T(128)} %param.11) | copy-start | bytes 100
  0.0 0.7 %copy-start.3 = (s32[256]{0:T(256)S(1)}, s32[256]{0:T(256)}, u32[]{:S(2)}) copy-start(s32[256]{0:T(256)} %param.13) | copy-start | bytes 3076
  0.0 0.7 %copy-start.4 = (s32[128]{0:T(128)S(1)}, s32[128]{0:T(128)}, u32[]{:S(2)}) copy-start(s32[128]{0:T(128)} %param.16) | copy-start | bytes 1540
  0.7 0.8 %copy-start = (bf16[256,128]{1,0:T(8,128)(2,1)S(1)}, bf16[256,128]{1,0:T(8,128)(2,1)}, u32[]{:S(2)}) copy-start(bf16[256,128]{1,0:T(8,128)(2,1)} %s_rows.1) | copy-start | bytes 196612
  1.6 0.8 %copy-start.1 = (bf16[128,128]{1,0:T(8,128)(2,1)S(1)}, bf16[128,128]{1,0:T(8,128)(2,1)}, u32[]{:S(2)}) copy-start(bf16[128,128]{1,0:T(8,128)(2,1)} %t_rows.1) | copy-start | bytes 98308
  2.3 0.8 %copy-start.2 = (bf16[128,128]{1,0:T(8,128)(2,1)S(1)}, bf16[128,128]{1,0:T(8,128)(2,1)}, u32[]{:S(2)}) copy-start(bf16[128,128]{1,0:T(8,128)(2,1)} %r_rows.1) | copy-start | bytes 98308

commit v3 on v2

--- a/solution.py
+++ b/solution.py
@@ -37,8 +37,38 @@
 
 
 def pack_kernel(
-    n_a, n_b, n_c, cap, s_rows, t_rows, s_keys, t_keys, r_keys, s_cnt, t_cnt, r_cnt, r_rows, out, r_out
+    n_a, n_b, n_c, cap,
+    s_rows, t_rows, r_rows, s_keys, t_keys, r_keys, s_cnt, t_cnt, r_cnt,
+    out, r_out,
+    s_keys_near, t_keys_near, r_keys_near, s_cnt_near, t_cnt_near, r_cnt_near, sem_small, sem_rows,
 ):
+    small = [
+        pltpu.make_async_copy(far, near, sem_small.at[i])
+        for i, (far, near) in enumerate(
+            (
+                (s_keys, s_keys_near),
+                (t_keys, t_keys_near),
+                (r_keys, r_keys_near),
+                (s_cnt, s_cnt_near),
+                (t_cnt, t_cnt_near),
+                (r_cnt, r_cnt_near),
+            )
+        )
+    ]
+    rows = []
+
+    def send(far, near):
+        rows.append(pltpu.make_async_copy(far, near, sem_rows.at[len(rows)]))
+
+    for a in range(n_a):
+        send(s_rows, out.at[pl.ds(a * n_b * n_c, n_b * n_c), pl.ds(0, cap), :])
+        for b in range(n_b):
+            d = (a * n_b + b) * n_c
+            send(t_rows.at[pl.ds(a * n_c, n_c)], out.at[pl.ds(d, n_c), pl.ds(cap, cap), :])
+    send(r_rows, r_out)
+    for copy in small + rows:
+        copy.start()
+
     def halves(keys_ref, cnt_ref):
         keys = keys_ref[...]
         slots = keys.shape[1]
@@ -46,23 +76,24 @@
         spread = (iota((groups, slots), 1) // cap == iota((groups, slots), 0)).astype(bf16)
         cnt = jnp.broadcast_to(cnt_ref[...].astype(f32).astype(bf16), (8, groups))
         live = (iota((1, slots), 1) % cap).astype(f32) < mm(cnt, spread)[0:1]
-        first = jnp.where(live, (keys // KEYS).astype(f32), -1.0)
-        second = jnp.where(live, (keys % KEYS).astype(f32), -1.0)
+        first = jnp.where(live, lax.div(keys, KEYS).astype(f32), -1.0)
+        second = jnp.where(live, lax.rem(keys, KEYS).astype(f32), -1.0)
         return first, second
 
     def at(vec, start):
         row = vec[:, start // LANES * LANES : (start // LANES + 1) * LANES]
         return pltpu.roll(row, (LANES - start % LANES) % LANES, 1) if start % LANES else row
 
-    r_out[...] = r_rows[...]
-    sb, sc = halves(s_keys, s_cnt)
-    ta, tc = halves(t_keys, t_cnt)
-    ra, rb = halves(r_keys, r_cnt)
+    for copy in small:
+        copy.wait()
+    sb, sc = halves(s_keys_near, s_cnt_near)
+    ta, tc = halves(t_keys_near, t_cnt_near)
+    ra, rb = halves(r_keys_near, r_cnt_near)
     seg = n_c * cap
     row = iota((META, LANES), 0)
     for a in range(n_a):
         for b in range(n_b):
-            rows = (
+            vecs = (
                 at(sb, b * seg),
                 at(sc, b * seg),
                 at(ta, a * seg),
@@ -71,15 +102,13 @@
                 at(rb, (a * n_b + b) * cap),
             )
             meta = jnp.zeros((META, LANES), f32)
-            for k, value in enumerate(rows):
+            for k, value in enumerate(vecs):
                 meta = jnp.where(row == k, value, meta)
             meta = meta.astype(bf16)
             for c in range(n_c):
-                d = (a * n_b + b) * n_c + c
-                g, h = b * n_c + c, a * n_c + c
-                out[d, 0:cap, :] = s_rows[g * cap : (g + 1) * cap, :]
-                out[d, cap : 2 * cap, :] = t_rows[h * cap : (h + 1) * cap, :]
-                out[d, 2 * cap : 2 * cap + META, :] = meta
+                out[(a * n_b + b) * n_c + c, 2 * cap : 2 * cap + META, :] = meta
+    for copy in rows:
+        copy.wait()
 
 
 def home_kernel(shares, r_rows, out):
@@ -173,16 +202,27 @@
     total_slots = n * cap
     wide = n_c * KEYS
     row = lambda x: x.reshape(1, x.shape[0])
+    far = lambda x: pltpu.with_memory_space_constraint(x, pltpu.HBM)
     near = lambda x: pltpu.with_memory_space_constraint(x, pltpu.VMEM)
     params = pltpu.CompilerParams(vmem_limit_bytes=40 << 20)
+    small = (row(s_keys), row(t_keys), row(r_keys), row(s_counts), row(t_counts), row(r_counts))
     packed, r_kept = pl.pallas_call(
         functools.partial(pack_kernel, n_a, n_b, n_c, cap),
+        in_specs=[pl.BlockSpec(memory_space=pltpu.HBM)] * 9,
         out_shape=(pltpu.VMEM((n, 2 * cap + META, width), bf16), pltpu.VMEM(r_rows.shape, bf16)),
+        scratch_shapes=[pltpu.VMEM(x.shape, x.dtype) for x in small]
+        + [
+            pltpu.SemaphoreType.DMA((len(small),)),
+            pltpu.SemaphoreType.DMA((n_a + n_a * n_b + 1,)),
+        ],
         compiler_params=params,
         name="pack",
     )(
-        s_rows, t_rows, row(s_keys), row(t_keys), row(r_keys),
-        row(s_counts), row(t_counts), row(r_counts), r_rows,
+        *map(
+            far,
+            (s_rows.reshape(n_b * n_c, cap, width), t_rows.reshape(n_a * n_c, cap, width), r_rows)
+            + small,
+        )
     )
     held = lax.all_to_all(packed, AXES, split_axis=0, concat_axis=0, tiled=True)
     shares = pl.pallas_call(

time: 38.6 us -> 36.3 us (0.940)
  local copies, waits for them, and re-layouts: 3.08 us -> 0 us
  Pallas kernels: 3.65 us -> 4.66 us
    unnamed x18 -> x0, local copies, waits for them, and re-layouts: 3.08 us -> none
    pallas_call x1, Pallas kernels: 0.21 us -> 1.23 us  [body(): pl.pallas_call(functools.partial(pack_kernel, n_a, n_b, n_c, cap), in_spe...]
where the time goes in v3:
time: 36.3 us; the launch traced here: 36.2 us
  blocking collectives  31.5 us (87%)
  Pallas kernels  4.66 us (13%)
    all_to_all x1, blocking collectives, body(): held = lax.all_to_all(packed, AXES, split_axis=0, concat_axis=0, tiled=True)  18.2 us
    all_to_all x1, blocking collectives, body(): back = lax.all_to_all(shares, AXES, split_axis=0, concat_axis=0, tiled=True)  13.3 us
    pallas_call x1, Pallas kernels, body(): pl.pallas_call(functools.partial(join_kernel, n_c, cap, srcs), out_shape=...  2.8 us
    pallas_call x1, Pallas kernels, body(): pl.pallas_call(functools.partial(pack_kernel, n_a, n_b, n_c, cap), in_spe...  1.23 us

profile of v3, /device:TPU:0, one launch (start us, length us, event | category | flops | bytes accessed | tf_op | source)
XLA Modules:
  0.0 36.2 jit_solution(16364752072543806938)
XLA Ops:
  0.0 1.2 %pack.1 = (bf16[32,40,128]{2,1,0:T(8,128)(2,1)S(1)}, bf16[128,128]{1,0:T(8,128)(2,1)S(1)}) custom-call(bf16[16,16,128]{2,1,0:T(8,128)(2,1)} %bitcast.10, bf16[8,16,128]{2,1,0:T(8,128)(2,1)} %bitcast.11, bf16[128,128]{1,0:T(8,128)(2,1)} %r_rows.1, s32[1,256]{1,0:T(1,128)} %bitcast.12, s32[1,128]{1,0:T(1,128)} %bitcast.13, s32[1,128]{1,0:T(1,128)} %bitcast.14, ...), custom_call_target="tpu_custom_call" | custom-call | tf_op jit(solution)/shard_map/pack/pallas_call | solution.py:209
  1.2 18.2 %all_to_all.10.held = bf16[32,40,128]{2,1,0:T(8,128)(2,1)S(1)} all-to-all(bf16[32,40,128]{2,1,0:T(8,128)(2,1)S(1)} %get-tuple-element.7), channel_id=1, replica_groups=mesh['aa'=2,'ba'=4,'col'=4] {'aa','ba','col'}, dimensions={0} | all-to-all | bytes 655360 | tf_op jit(solution)/shard_map/all_to_all | solution.py:227
  19.4 2.8 %join.1 = f32[32,16,128]{2,1,0:T(8,128)S(1)} custom-call(bf16[32,40,128]{2,1,0:T(8,128)(2,1)S(1)} %all_to_all.10.held), custom_call_target="tpu_custom_call" | custom-call | tf_op jit(solution)/shard_map/join/pallas_call | solution.py:228
  22.2 13.3 %all_to_all.11 = f32[32,16,128]{2,1,0:T(8,128)S(1)} all-to-all(f32[32,16,128]{2,1,0:T(8,128)S(1)} %join.1), channel_id=1, replica_groups=mesh['aa'=2,'ba'=4,'col'=4] {'aa','ba','col'}, dimensions={0} | all-to-all | bytes 524288 | tf_op jit(solution)/shard_map/all_to_all | solution.py:236
  35.5 0.6 %home.1 = bf16[128,128]{1,0:T(8,128)(2,1)} custom-call(f32[8,4,16,128]{3,2,1,0:T(8,128)S(1)} %bitcast.9, bf16[128,128]{1,0:T(8,128)(2,1)S(1)} %get-tuple-element.8.r_rows), custom_call_target="tpu_custom_call" | custom-call | tf_op jit(solution)/shard_map/home/pallas_call | solution.py:237

commit v4 on v3

v4 whole, which is shorter than its diff:
```python
import functools

import jax
import jax.numpy as jnp
from jax import lax
from jax.experimental import pallas as pl
from jax.experimental.pallas import tpu as pltpu
from jax.sharding import PartitionSpec as P

KEYS = 64
LANES = 128
META = 8
AXES = ("aa", "ba", "col")
f32 = jnp.float32
bf16 = jnp.bfloat16


def iota(shape, dim):
    return lax.broadcasted_iota(jnp.int32, shape, dim)


def split(x):
    hi = x.astype(bf16)
    return hi, (x - hi.astype(f32)).astype(bf16)


def mm(x, y):
    return lax.dot_general(x, y, (((1,), (0,)), ((), ())), preferred_element_type=f32)


def mm_nt(x, y):
    return lax.dot_general(x, y, (((1,), (1,)), ((), ())), preferred_element_type=f32)


def mm_tn(x, y):
    return lax.dot_general(x, y, (((0,), (0,)), ((), ())), preferred_element_type=f32)


def swap(x, y):
    half = x.shape[-1] // 2
    low = iota(x.shape, x.ndim - 1) < half
    turn = lambda v: pltpu.roll(v, half, v.ndim - 1)
    return jnp.where(low, x, turn(y)), jnp.where(low, turn(x), y)


def pack_kernel(
    n_a, n_b, n_c, cap, split_w,
    s_rows, t_rows, r_rows, s_keys, t_keys, r_keys, s_cnt, t_cnt, r_cnt,
    out, r_out,
    s_near, t_near,
    s_keys_near, t_keys_near, r_keys_near, s_cnt_near, t_cnt_near, r_cnt_near, sem,
):
    small = [
        pltpu.make_async_copy(far, near, sem.at[i])
        for i, (far, near) in enumerate(
            (
                (s_keys, s_keys_near),
                (t_keys, t_keys_near),
                (r_keys, r_keys_near),
                (s_cnt, s_cnt_near),
                (t_cnt, t_cnt_near),
                (r_cnt, r_cnt_near),
            )
        )
    ]
    rows = [
        pltpu.make_async_copy(far, near, sem.at[len(small) + i])
        for i, (far, near) in enumerate(((s_rows, s_near), (t_rows, t_near), (r_rows, r_out)))
    ]
    for copy in small + rows:
        copy.start()

    def halves(keys_ref, cnt_ref):
        keys = keys_ref[...]
        slots = keys.shape[1]
        groups = slots // cap
        spread = (iota((groups, slots), 1) // cap == iota((groups, slots), 0)).astype(bf16)
        cnt = jnp.broadcast_to(cnt_ref[...].astype(f32).astype(bf16), (8, groups))
        live = (iota((1, slots), 1) % cap).astype(f32) < mm(cnt, spread)[0:1]
        first = jnp.where(live, lax.div(keys, KEYS).astype(f32), -1.0)
        second = jnp.where(live, lax.rem(keys, KEYS).astype(f32), -1.0)
        return first, second

    def at(vec, start):
        row = vec[:, start // LANES * LANES : (start // LANES + 1) * LANES]
        return pltpu.roll(row, (LANES - start % LANES) % LANES, 1) if start % LANES else row

    for copy in small:
        copy.wait()
    sb, sc = halves(s_keys_near, s_cnt_near)
    ta, tc = halves(t_keys_near, t_cnt_near)
    ra, rb = halves(r_keys_near, r_cnt_near)
    seg = n_c * cap
    row = iota((META, LANES), 0)

    def ring(vec, start):
        out = at(vec, start)
        size = seg
        while size < LANES:
            out = jnp.where(iota((1, LANES), 1) < size, out, pltpu.roll(out, size, 1))
            size *= 2
        return out

    s_meta = [(ring(sb, b * seg), ring(sc, b * seg)) for b in range(n_b)]
    t_meta = [(ring(ta, a * seg), ring(tc, a * seg)) for a in range(n_a)]
    for a in range(n_a):
        for b in range(n_b):
            meta = jnp.zeros((META, LANES), f32)
            for k, value in enumerate(s_meta[b] + t_meta[a]):
                meta = jnp.where(row == k, value, meta)
            r_at = (a * n_b + b) * cap
            for c in range(0, n_c, split_w):
                turned = pltpu.roll(meta, LANES - c * cap, 1) if c else meta
                for k, vec in ((4, ra), (5, rb)):
                    turned = jnp.where(row == k, at(vec, r_at), turned)
                turned = turned.astype(bf16)
                for w in range(split_w):
                    out[(a * n_b + b) * n_c + c + w, 2 * cap : 2 * cap + META, :] = turned
    for copy in rows:
        copy.wait()

    def parts(near, g):
        if split_w == 1:
            return (near[g],)
        pair = swap(near[g].astype(f32), near[g + 1].astype(f32))
        return tuple(x.astype(bf16) for x in pair)

    for c in range(0, n_c, split_w):
        for b in range(n_b):
            for w, part in enumerate(parts(s_near, b * n_c + c)):
                for a in range(n_a):
                    out[(a * n_b + b) * n_c + c + w, 0:cap, :] = part
        for a in range(n_a):
            for w, part in enumerate(parts(t_near, a * n_c + c)):
                for b in range(n_b):
                    out[(a * n_b + b) * n_c + c + w, cap : 2 * cap, :] = part


def home_kernel(split_w, shares, r_rows, out):
    groups, n_c, cap_w, width = shares.shape
    total = [shares[:, w] for w in range(split_w)]
    for c in range(split_w, n_c):
        total[c % split_w] = total[c % split_w] + shares[:, c]
    if split_w == 2:
        total = swap(*total)
    for w in range(split_w):
        at = pl.ds(w * cap_w, cap_w)
        out[:, at, :] = (r_rows[:, at, :].astype(f32) * total[w]).astype(bf16)


BIG = 2.0**15


def join_kernel(n_c, cap, split_w, srcs, held, out, sb_ref, sc_ref, ta_ref, tc_ref, f_ref):
    blocks = held.shape[0] // srcs
    m = srcs * cap
    key_in = lambda shape, dim: (iota(shape, dim) % KEYS).astype(f32)
    place = iota((cap, LANES), 1) % cap == iota((cap, LANES), 0)
    order_c = [i for i in range(split_w) for _ in range(2)] + list(range(split_w, n_c))
    order_c += [-2] * (len(order_c) % 2)
    order_b = list(range(n_c)) + [-1] * (n_c % 2)
    wide_b, wide_c = len(order_b) * KEYS, len(order_c) * KEYS

    def bucket(order, shape, dim):
        block = iota(shape, dim) // KEYS
        at = jnp.full(shape, order[0], jnp.int32)
        for k in range(1, len(order)):
            at = jnp.where(block == k, order[k], at)
        return at

    lane_b = iota((LANES, wide_b), 0) // cap
    lane_c = iota((LANES, wide_c), 0) // cap
    sel_b = (lane_b == bucket(order_b, (LANES, wide_b), 1)).astype(bf16)
    sel_c = (lane_c == bucket(order_c, (LANES, wide_c), 1)).astype(bf16)
    sel_r = (iota((LANES, LANES), 0) < cap).astype(bf16)

    def onehot(meta, kind, sel):
        rep = jnp.broadcast_to(meta[:, kind : kind + 1, :], (srcs, cap, LANES))
        rep = jnp.where(place[None], rep, 0.0).astype(bf16).reshape(m, LANES)
        return mm(rep, sel) == key_in((m, sel.shape[1]), 1)

    def meta_of(i):
        return held[pl.ds(i * srcs, srcs), 2 * cap : 2 * cap + META, :].astype(f32)

    own_b, own_c = LANES, split_w * LANES

    def tables(i):
        meta = meta_of(i)
        at = pl.ds(i * m, m)
        for k, (b_ref, c_ref) in enumerate(((sb_ref, sc_ref), (ta_ref, tc_ref))):
            b = onehot(meta, 2 * k, sel_b).astype(bf16)
            c = onehot(meta, 2 * k + 1, sel_c).astype(bf16)
            f_ref[k] += mm_tn(b, c)
            b_ref[at] = b[:, 0:own_b]
            c_ref[at] = c[:, 0:own_c]

    def counts(k):
        total = jnp.zeros((KEYS, wide_c), f32)
        at = bucket(order_c, (KEYS, wide_c), 1)
        for j, b in enumerate(order_b):
            total = total + jnp.where(at == b, f_ref[k, pl.ds(j * KEYS, KEYS), :], 0.0)
        return total

    def joins(gather_a, gather_b, i):
        meta = meta_of(i)
        ra = onehot(meta, 4, sel_r)
        rb = onehot(meta, 5, sel_r)
        va = mm(ra.astype(bf16), gather_a)
        vb = mm(rb.astype(bf16), gather_b)
        pick = [
            jnp.where(rb, va[:, k * LANES : (k + 1) * LANES], 0.0).astype(bf16)
            for k in range(split_w, split_w + 2)
        ]
        scale = mm(jnp.concatenate(pick, 1), jnp.ones((2 * LANES, LANES), bf16))
        low = iota((m, LANES), 1) < KEYS

        def sides(value, hot):
            flag = jnp.where(hot, BIG, 0.0)
            return [
                jnp.concatenate(
                    [
                        value[:, w * LANES : (w + 1) * LANES].astype(bf16),
                        jnp.where(low == (w == 0), flag, 0.0).astype(bf16),
                    ],
                    1,
                )
                for w in range(split_w)
            ]

        of_s, of_t = sides(va, rb), sides(vb, ra)

        def one(j, accs):
            at = pl.ds(j * m, m)
            rows = held[pl.ds(j * srcs, srcs), 0 : 2 * cap, :]
            accs = list(accs)
            for left, b_ref, c_ref, start in ((of_s, sb_ref, sc_ref, 0), (of_t, ta_ref, tc_ref, cap)):
                x = rows[:, start : start + cap, :].reshape(m, LANES)
                b = b_ref[at]
                for w in range(split_w):
                    right = jnp.concatenate([c_ref[at, w * LANES : (w + 1) * LANES], b], 1)
                    hi, lo = split(jnp.maximum(mm_nt(left[w], right) - BIG, 0.0))
                    accs[w] = accs[w] + mm(hi, x) + mm(lo, x)
            return tuple(accs)

        accs = tuple(jnp.zeros((m, LANES), f32) for _ in range(split_w))
        accs = one(0, accs) if blocks == 1 else lax.fori_loop(0, blocks, one, accs)
        accs = [(acc * scale).reshape(srcs, cap, LANES) for acc in accs]
        at = pl.ds(i * srcs, srcs)
        if split_w == 1:
            out[at] = accs[0]
        else:
            half = cap // 2
            turn = lambda v: pltpu.roll(v, LANES // 2, 2)
            first = accs[0][:, :half] + turn(accs[1][:, :half])
            second = turn(accs[0][:, half:]) + accs[1][:, half:]
            out[at] = jnp.where(iota((srcs, half, LANES), 2) < LANES // 2, first, second)

    def each(step):
        if blocks == 1:
            step(0)
        else:
            pl.loop(0, blocks)(step)

    f_ref[...] = jnp.zeros_like(f_ref)
    each(tables)
    s_counts, t_counts = counts(0), counts(1)
    once = (iota((KEYS, wide_c), 1) // KEYS % 2 == 0) | (iota((KEYS, wide_c), 1) >= own_c)
    s_parts, t_parts = split(s_counts), split(jnp.where(once, t_counts, 0.0))
    triangles = sum(mm_nt(t, s) for t in t_parts for s in s_parts)
    scale = 1.0 / jnp.sqrt(1.0 + triangles)
    hi, rest = split(scale)
    middle, rest = split(scale - hi.astype(f32))
    left = lambda x: iota(x.shape, 1) < KEYS

    def gather(count, tail):
        hi, lo = split(count[:, 0:own_c])
        first = iota(hi.shape, 1) % LANES < KEYS
        table = jnp.concatenate([jnp.where(first, hi.astype(f32), lo.astype(f32)), *tail], 1)
        table = table.astype(bf16)
        return jnp.concatenate([table, jnp.zeros_like(table)], 0)

    parts = [x.astype(f32) for x in (hi, middle, rest)] + [jnp.zeros((KEYS, KEYS), f32)]
    each(functools.partial(joins, gather(t_counts, parts), gather(s_counts, [])))


def body(sizes, r_rows, r_keys, r_counts, s_rows, s_keys, s_counts, t_rows, t_keys, t_counts):
    n_a, n_b, n_c = sizes
    n = n_a * n_b * n_c
    cap = r_keys.shape[0] // r_counts.shape[0]
    width = r_rows.shape[1]
    srcs = max(512 // cap, 1)
    srcs = srcs if n % srcs == 0 else n
    total_slots = n * cap
    split_w = 2 if n_c % 2 == 0 and width == LANES and cap % 16 == 0 else 1
    wide_b, wide_c = -(-n_c // 2) * LANES, -(-(n_c + split_w) // 2) * LANES
    row = lambda x: x.reshape(1, x.shape[0])
    far = lambda x: pltpu.with_memory_space_constraint(x, pltpu.HBM)
    near = lambda x: pltpu.with_memory_space_constraint(x, pltpu.VMEM)
    params = pltpu.CompilerParams(vmem_limit_bytes=40 << 20)
    small = (row(s_keys), row(t_keys), row(r_keys), row(s_counts), row(t_counts), row(r_counts))
    groups = (s_rows.shape[0] // cap, t_rows.shape[0] // cap, r_rows.shape[0] // cap)
    blocked = [x.reshape(g, cap, width) for x, g in zip((s_rows, t_rows, r_rows), groups)]
    near_like = lambda x: pltpu.VMEM(x.shape, x.dtype)
    packed, r_kept = pl.pallas_call(
        functools.partial(pack_kernel, n_a, n_b, n_c, cap, split_w),
        in_specs=[pl.BlockSpec(memory_space=pltpu.HBM)] * 9,
        out_shape=(pltpu.VMEM((n, 2 * cap + META, width), bf16), near_like(blocked[2])),
        scratch_shapes=[near_like(x) for x in (*blocked[:2], *small)]
        + [pltpu.SemaphoreType.DMA((9,))],
        compiler_params=params,
        name="pack",
    )(*map(far, (*blocked, *small)))
    held = lax.all_to_all(packed, AXES, split_axis=0, concat_axis=0, tiled=True)
    shares = pl.pallas_call(
        functools.partial(join_kernel, n_c, cap, split_w, srcs),
        out_shape=pltpu.VMEM((n, cap // split_w, width), f32),
        scratch_shapes=[
            pltpu.VMEM((total_slots, LANES), bf16),
            pltpu.VMEM((total_slots, split_w * LANES), bf16),
        ]
        * 2
        + [pltpu.VMEM((2, wide_b, wide_c), f32)],
        compiler_params=params,
        name="join",
    )(near(held))
    back = lax.all_to_all(shares, AXES, split_axis=0, concat_axis=0, tiled=True)
    joined = pl.pallas_call(
        functools.partial(home_kernel, split_w),
        out_shape=jax.ShapeDtypeStruct(blocked[2].shape, bf16),
        compiler_params=params,
        name="home",
    )(near(back.reshape(n_a * n_b, n_c, cap // split_w, width)), near(r_kept))
    return joined.reshape(r_rows.shape)


def solution(mesh):
    rows, flat = P(AXES, None), P(AXES)
    sizes = tuple(mesh.shape[name] for name in AXES)
    return jax.shard_map(
        functools.partial(body, sizes),
        mesh=mesh,
        in_specs=(rows, flat, flat) * 3,
        out_specs=rows,
        check_vma=False,
    )
```

time: 36.3 us -> 35.5 us (0.978)
  blocking collectives: 31.5 us -> 29.6 us
  Pallas kernels: 4.66 us -> 5.67 us
    all_to_all x1, blocking collectives: 13.3 us -> 11.4 us  [body(): back = lax.all_to_all(shares, AXES, split_axis=0, concat_axis=0, tiled=True)]
    pallas_call x3, Pallas kernels: 4.66 us -> 5.67 us  [the longest x1 3.71 us: body(): pl.pallas_call(functools.partial(join_kernel, n_c, cap, split_w, srcs), o...]
where the time goes in v4:
time: 35.5 us; the launch traced here: 35.3 us
  blocking collectives  29.6 us (83%)
  Pallas kernels  5.67 us (16%)
    all_to_all x1, blocking collectives, body(): held = lax.all_to_all(packed, AXES, split_axis=0, concat_axis=0, tiled=True)  18.2 us
    all_to_all x1, blocking collectives, body(): back = lax.all_to_all(shares, AXES, split_axis=0, concat_axis=0, tiled=True)  11.4 us
    pallas_call x1, Pallas kernels, body(): pl.pallas_call(functools.partial(join_kernel, n_c, cap, split_w, srcs), o...  3.71 us
    pallas_call x1, Pallas kernels, body(): pl.pallas_call(functools.partial(pack_kernel, n_a, n_b, n_c, cap, split_w...  1.26 us

profile of v4, /device:TPU:0, one launch (start us, length us, event | category | flops | bytes accessed | tf_op | source)
XLA Modules:
  0.0 35.3 jit_solution(17076662988249567750)
XLA Ops:
  0.0 1.3 %pack.1 = (bf16[32,40,128]{2,1,0:T(8,128)(2,1)S(1)}, bf16[8,16,128]{2,1,0:T(8,128)(2,1)S(1)}) custom-call(bf16[16,16,128]{2,1,0:T(8,128)(2,1)} %bitcast.12, bf16[8,16,128]{2,1,0:T(8,128)(2,1)} %bitcast.13, bf16[8,16,128]{2,1,0:T(8,128)(2,1)} %bitcast.14, s32[1,256]{1,0:T(1,128)} %bitcast.15, s32[1,128]{1,0:T(1,128)} %bitcast.16, s32[1,128]{1,0:T(1,128)} %bitcast.17, ...), custom_call_target="tpu_custom_call" | custom-call | tf_op jit(solution)/shard_map/pack/pallas_call | solution.py:304
  1.3 18.2 %all_to_all.10.held = bf16[32,40,128]{2,1,0:T(8,128)(2,1)S(1)} all-to-all(bf16[32,40,128]{2,1,0:T(8,128)(2,1)S(1)} %get-tuple-element.7), channel_id=1, replica_groups=mesh['aa'=2,'ba'=4,'col'=4] {'aa','ba','col'}, dimensions={0} | all-to-all | bytes 655360 | tf_op jit(solution)/shard_map/all_to_all | solution.py:313
  19.5 3.7 %join.1 = f32[32,8,128]{2,1,0:T(8,128)S(1)} custom-call(bf16[32,40,128]{2,1,0:T(8,128)(2,1)S(1)} %all_to_all.10.held), custom_call_target="tpu_custom_call" | custom-call | tf_op jit(solution)/shard_map/join/pallas_call | solution.py:314
  23.2 11.4 %all_to_all.11 = f32[32,8,128]{2,1,0:T(8,128)S(1)} all-to-all(f32[32,8,128]{2,1,0:T(8,128)S(1)} %join.1), channel_id=1, replica_groups=mesh['aa'=2,'ba'=4,'col'=4] {'aa','ba','col'}, dimensions={0} | all-to-all | bytes 262144 | tf_op jit(solution)/shard_map/all_to_all | solution.py:326
  34.6 0.7 %home.1 = bf16[8,16,128]{2,1,0:T(8,128)(2,1)} custom-call(f32[8,4,8,128]{3,2,1,0:T(8,128)S(1)} %bitcast.11, bf16[8,16,128]{2,1,0:T(8,128)(2,1)S(1)} %get-tuple-element.8.r_rows), custom_call_target="tpu_custom_call" | custom-call | tf_op jit(solution)/shard_map/home/pallas_call | solution.py:327

commit v5 on v4

--- a/solution.py
+++ b/solution.py
@@ -149,111 +149,101 @@
 
 
 BIG = 2.0**15
-
-
-def join_kernel(n_c, cap, split_w, srcs, held, out, sb_ref, sc_ref, ta_ref, tc_ref, f_ref):
+EXACT = 256.0
+
+
+def join_kernel(n_c, cap, split_w, srcs, held, out, s_ref, t_ref, f_ref):
     blocks = held.shape[0] // srcs
     m = srcs * cap
+    wide = f_ref.shape[1]
+    rows_of = LANES // split_w
+    part = cap // split_w
     key_in = lambda shape, dim: (iota(shape, dim) % KEYS).astype(f32)
     place = iota((cap, LANES), 1) % cap == iota((cap, LANES), 0)
-    order_c = [i for i in range(split_w) for _ in range(2)] + list(range(split_w, n_c))
-    order_c += [-2] * (len(order_c) % 2)
-    order_b = list(range(n_c)) + [-1] * (n_c % 2)
-    wide_b, wide_c = len(order_b) * KEYS, len(order_c) * KEYS
-
-    def bucket(order, shape, dim):
-        block = iota(shape, dim) // KEYS
-        at = jnp.full(shape, order[0], jnp.int32)
-        for k in range(1, len(order)):
-            at = jnp.where(block == k, order[k], at)
-        return at
-
-    lane_b = iota((LANES, wide_b), 0) // cap
-    lane_c = iota((LANES, wide_c), 0) // cap
-    sel_b = (lane_b == bucket(order_b, (LANES, wide_b), 1)).astype(bf16)
-    sel_c = (lane_c == bucket(order_c, (LANES, wide_c), 1)).astype(bf16)
-    sel_r = (iota((LANES, LANES), 0) < cap).astype(bf16)
-
-    def onehot(meta, kind, sel):
-        rep = jnp.broadcast_to(meta[:, kind : kind + 1, :], (srcs, cap, LANES))
-        rep = jnp.where(place[None], rep, 0.0).astype(bf16).reshape(m, LANES)
-        return mm(rep, sel) == key_in((m, sel.shape[1]), 1)
+    sel = (iota((LANES, wide), 0) // cap == iota((LANES, wide), 1) // KEYS).astype(bf16)
 
     def meta_of(i):
         return held[pl.ds(i * srcs, srcs), 2 * cap : 2 * cap + META, :].astype(f32)
 
-    own_b, own_c = LANES, split_w * LANES
-
     def tables(i):
         meta = meta_of(i)
+
+        def hot(kind):
+            rep = jnp.broadcast_to(meta[:, kind : kind + 1, :], (srcs, cap, LANES))
+            rep = jnp.where(place[None], rep, 0.0).astype(bf16).reshape(m, LANES)
+            return (mm(rep, sel) == key_in((m, wide), 1)).astype(bf16)
+
         at = pl.ds(i * m, m)
-        for k, (b_ref, c_ref) in enumerate(((sb_ref, sc_ref), (ta_ref, tc_ref))):
-            b = onehot(meta, 2 * k, sel_b).astype(bf16)
-            c = onehot(meta, 2 * k + 1, sel_c).astype(bf16)
-            f_ref[k] += mm_tn(b, c)
-            b_ref[at] = b[:, 0:own_b]
-            c_ref[at] = c[:, 0:own_c]
+        for k, ref in enumerate((s_ref, t_ref)):
+            first, c = hot(2 * k), hot(2 * k + 1)
+            if blocks == 1:
+                f_ref[k] = mm_tn(first, c)
+            else:
+                f_ref[k] += mm_tn(first, c)
+            ref[at, 0:LANES] = c[:, 0:LANES]
+            ref[at, LANES : 2 * LANES] = first[:, 0:LANES]
 
     def counts(k):
-        total = jnp.zeros((KEYS, wide_c), f32)
-        at = bucket(order_c, (KEYS, wide_c), 1)
-        for j, b in enumerate(order_b):
-            total = total + jnp.where(at == b, f_ref[k, pl.ds(j * KEYS, KEYS), :], 0.0)
+        block = iota((KEYS, wide), 1) // KEYS
+        total = f_ref[k, 0:KEYS, :]
+        for j in range(1, wide // KEYS):
+            total = jnp.where(block == j, f_ref[k, j * KEYS : (j + 1) * KEYS, :], total)
         return total
 
-    def joins(gather_a, gather_b, i):
+    def r_hot(meta, kind):
+        row = jnp.broadcast_to(meta[:, kind : kind + 1, :], (srcs, part, LANES))
+        lane, at = iota((part, LANES), 1), iota((part, LANES), 0)
+        key = [
+            jnp.sum(jnp.where((lane == at + w * part)[None], row, 0.0), axis=2, keepdims=True)
+            for w in range(split_w)
+        ]
+        key = jnp.concatenate([x.reshape(srcs * part, 1) for x in key], 0)
+        return key == key_in((m, LANES), 1)
+
+    def joins(s_table, t_table, s_more, t_more, more, i):
         meta = meta_of(i)
-        ra = onehot(meta, 4, sel_r)
-        rb = onehot(meta, 5, sel_r)
-        va = mm(ra.astype(bf16), gather_a)
-        vb = mm(rb.astype(bf16), gather_b)
-        pick = [
-            jnp.where(rb, va[:, k * LANES : (k + 1) * LANES], 0.0).astype(bf16)
-            for k in range(split_w, split_w + 2)
-        ]
-        scale = mm(jnp.concatenate(pick, 1), jnp.ones((2 * LANES, LANES), bf16))
-        low = iota((m, LANES), 1) < KEYS
+        ra = r_hot(meta, 4)
+        rb = r_hot(meta, 5)
+        half = iota((m, LANES), 1) // KEYS
+        ra16, rb16 = ra.astype(bf16), rb.astype(bf16)
+        va, vb = mm(ra16, t_table), mm(rb16, s_table)
+        pick = va[:, LANES : 2 * LANES] + va[:, 2 * LANES : 3 * LANES]
+        scale = jnp.sum(jnp.where(rb, pick, 0.0), axis=1, keepdims=True)
 
         def sides(value, hot):
-            flag = jnp.where(hot, BIG, 0.0)
+            both = (value[:, 0:LANES], jnp.where(hot, 0.0, -BIG))
             return [
-                jnp.concatenate(
-                    [
-                        value[:, w * LANES : (w + 1) * LANES].astype(bf16),
-                        jnp.where(low == (w == 0), flag, 0.0).astype(bf16),
-                    ],
-                    1,
-                )
+                jnp.concatenate([jnp.where(half == w, x, 0.0).astype(bf16) for x in both], 1)
                 for w in range(split_w)
             ]
 
-        of_s, of_t = sides(va, rb), sides(vb, ra)
-
-        def one(j, accs):
+        def one(of_s, of_t, j, acc):
             at = pl.ds(j * m, m)
             rows = held[pl.ds(j * srcs, srcs), 0 : 2 * cap, :]
-            accs = list(accs)
-            for left, b_ref, c_ref, start in ((of_s, sb_ref, sc_ref, 0), (of_t, ta_ref, tc_ref, cap)):
-                x = rows[:, start : start + cap, :].reshape(m, LANES)
-                b = b_ref[at]
+            xs, matches = [], []
+            for left, ref, start in ((of_s, s_ref, 0), (of_t, t_ref, cap)):
+                x = rows[:, start : start + cap, :].reshape(m, LANES).T
+                right = ref[at]
                 for w in range(split_w):
-                    right = jnp.concatenate([c_ref[at, w * LANES : (w + 1) * LANES], b], 1)
-                    hi, lo = split(jnp.maximum(mm_nt(left[w], right) - BIG, 0.0))
-                    accs[w] = accs[w] + mm(hi, x) + mm(lo, x)
-            return tuple(accs)
-
-        accs = tuple(jnp.zeros((m, LANES), f32) for _ in range(split_w))
-        accs = one(0, accs) if blocks == 1 else lax.fori_loop(0, blocks, one, accs)
-        accs = [(acc * scale).reshape(srcs, cap, LANES) for acc in accs]
-        at = pl.ds(i * srcs, srcs)
-        if split_w == 1:
-            out[at] = accs[0]
-        else:
-            half = cap // 2
-            turn = lambda v: pltpu.roll(v, LANES // 2, 2)
-            first = accs[0][:, :half] + turn(accs[1][:, :half])
-            second = turn(accs[0][:, half:]) + accs[1][:, half:]
-            out[at] = jnp.where(iota((srcs, half, LANES), 2) < LANES // 2, first, second)
+                    xs.append(x[w * rows_of : (w + 1) * rows_of])
+                    matches.append(jnp.maximum(mm_nt(right, left[w]), 0.0).astype(bf16))
+            return acc + mm(jnp.concatenate(xs, 1), jnp.concatenate(matches, 0))
+
+        def over(of_s, of_t, acc):
+            step = functools.partial(one, of_s, of_t)
+            return step(0, acc) if blocks == 1 else lax.fori_loop(0, blocks, step, acc)
+
+        acc = over(sides(va, rb), sides(vb, ra), jnp.zeros((rows_of, m), f32))
+        again = lambda x: over(sides(mm(ra16, t_more), rb), sides(mm(rb16, s_more), ra), x)
+        acc = lax.cond(more, again, lambda x: x, acc)
+        size = srcs * part
+        acc = jnp.concatenate([acc[:, w * size : (w + 1) * size] for w in range(split_w)], 0).T
+        factor = scale[0:size]
+        for w in range(1, split_w):
+            factor = jnp.where(
+                iota((size, LANES), 1) < w * rows_of, factor, scale[w * size : (w + 1) * size]
+            )
+        out[pl.ds(i * srcs, srcs)] = (acc * factor).reshape(srcs, part, LANES)
 
     def each(step):
         if blocks == 1:
@@ -261,26 +251,36 @@
         else:
             pl.loop(0, blocks)(step)
 
-    f_ref[...] = jnp.zeros_like(f_ref)
+    if blocks > 1:
+        f_ref[...] = jnp.zeros_like(f_ref)
     each(tables)
     s_counts, t_counts = counts(0), counts(1)
-    once = (iota((KEYS, wide_c), 1) // KEYS % 2 == 0) | (iota((KEYS, wide_c), 1) >= own_c)
-    s_parts, t_parts = split(s_counts), split(jnp.where(once, t_counts, 0.0))
-    triangles = sum(mm_nt(t, s) for t in t_parts for s in s_parts)
+    triangles = sum(mm_nt(t, s) for t in split(t_counts) for s in split(s_counts))
     scale = 1.0 / jnp.sqrt(1.0 + triangles)
-    hi, rest = split(scale)
+    hi, _ = split(scale)
     middle, rest = split(scale - hi.astype(f32))
-    left = lambda x: iota(x.shape, 1) < KEYS
-
-    def gather(count, tail):
-        hi, lo = split(count[:, 0:own_c])
-        first = iota(hi.shape, 1) % LANES < KEYS
-        table = jnp.concatenate([jnp.where(first, hi.astype(f32), lo.astype(f32)), *tail], 1)
-        table = table.astype(bf16)
-        return jnp.concatenate([table, jnp.zeros_like(table)], 0)
-
-    parts = [x.astype(f32) for x in (hi, middle, rest)] + [jnp.zeros((KEYS, KEYS), f32)]
-    each(functools.partial(joins, gather(t_counts, parts), gather(s_counts, [])))
+
+    def parts(count):
+        count = count[:, 0:LANES]
+        high = jnp.floor(count / EXACT) * EXACT
+        return count - high, high
+
+    def table(*columns):
+        x = jnp.concatenate([c.astype(f32) for c in columns], 1).astype(bf16)
+        return jnp.concatenate([x, jnp.zeros_like(x)], 0)
+
+    s_low, s_high = parts(s_counts)
+    t_low, t_high = parts(t_counts)
+    each(
+        functools.partial(
+            joins,
+            table(s_low),
+            table(t_low, hi, middle, rest, jnp.zeros((KEYS, KEYS), f32)),
+            table(s_high),
+            table(t_high),
+            jnp.maximum(jnp.max(s_high), jnp.max(t_high)) > 0.0,
+        )
+    )
 
 
 def body(sizes, r_rows, r_keys, r_counts, s_rows, s_keys, s_counts, t_rows, t_keys, t_counts):
@@ -292,7 +292,7 @@
     srcs = srcs if n % srcs == 0 else n
     total_slots = n * cap
     split_w = 2 if n_c % 2 == 0 and width == LANES and cap % 16 == 0 else 1
-    wide_b, wide_c = -(-n_c // 2) * LANES, -(-(n_c + split_w) // 2) * LANES
+    wide = -(-n_c // 2) * LANES
     row = lambda x: x.reshape(1, x.shape[0])
     far = lambda x: pltpu.with_memory_space_constraint(x, pltpu.HBM)
     near = lambda x: pltpu.with_memory_space_constraint(x, pltpu.VMEM)
@@ -314,12 +314,8 @@
     shares = pl.pallas_call(
         functools.partial(join_kernel, n_c, cap, split_w, srcs),
         out_shape=pltpu.VMEM((n, cap // split_w, width), f32),
-        scratch_shapes=[
-            pltpu.VMEM((total_slots, LANES), bf16),
-            pltpu.VMEM((total_slots, split_w * LANES), bf16),
-        ]
-        * 2
-        + [pltpu.VMEM((2, wide_b, wide_c), f32)],
+        scratch_shapes=[pltpu.VMEM((total_slots, 2 * LANES), bf16)] * 2
+        + [pltpu.VMEM((2, wide, wide), f32)],
         compiler_params=params,
         name="join",
     )(near(held))

time: 35.5 us -> 34.2 us (0.963)
  Pallas kernels: 5.67 us -> 4.36 us
    pallas_call x1, Pallas kernels: 3.71 us -> 2.4 us  [body(): pl.pallas_call(functools.partial(join_kernel, n_c, cap, split_w, srcs), o...]
where the time goes in v5:
time: 34.2 us; the launch traced here: 34 us
  blocking collectives  29.6 us (87%)
  Pallas kernels  4.36 us (13%)
    all_to_all x1, blocking collectives, body(): held = lax.all_to_all(packed, AXES, split_axis=0, concat_axis=0, tiled=True)  18.2 us
    all_to_all x1, blocking collectives, body(): back = lax.all_to_all(shares, AXES, split_axis=0, concat_axis=0, tiled=True)  11.4 us
    pallas_call x1, Pallas kernels, body(): pl.pallas_call(functools.partial(join_kernel, n_c, cap, split_w, srcs), o...  2.4 us
    pallas_call x1, Pallas kernels, body(): pl.pallas_call(functools.partial(pack_kernel, n_a, n_b, n_c, cap, split_w...  1.26 us
    pallas_call x1, Pallas kernels, body(): pl.pallas_call(functools.partial(home_kernel, split_w), out_shape=jax.Sha...  0.7 us

profile of v5, /device:TPU:0, one launch (start us, length us, event | category | flops | bytes accessed | tf_op | source)
XLA Modules:
  0.0 34.0 jit_solution(548527151942774029)
XLA Ops:
  0.0 1.3 %pack.1 = (bf16[32,40,128]{2,1,0:T(8,128)(2,1)S(1)}, bf16[8,16,128]{2,1,0:T(8,128)(2,1)S(1)}) custom-call(bf16[16,16,128]{2,1,0:T(8,128)(2,1)} %bitcast.12, bf16[8,16,128]{2,1,0:T(8,128)(2,1)} %bitcast.13, bf16[8,16,128]{2,1,0:T(8,128)(2,1)} %bitcast.14, s32[1,256]{1,0:T(1,128)} %bitcast.15, s32[1,128]{1,0:T(1,128)} %bitcast.16, s32[1,128]{1,0:T(1,128)} %bitcast.17, ...), custom_call_target="tpu_custom_call" | custom-call | tf_op jit(solution)/shard_map/pack/pallas_call | solution.py:304
  1.3 18.2 %all_to_all.10.held = bf16[32,40,128]{2,1,0:T(8,128)(2,1)S(1)} all-to-all(bf16[32,40,128]{2,1,0:T(8,128)(2,1)S(1)} %get-tuple-element.7), channel_id=1, replica_groups=mesh['aa'=2,'ba'=4,'col'=4] {'aa','ba','col'}, dimensions={0} | all-to-all | bytes 655360 | tf_op jit(solution)/shard_map/all_to_all | solution.py:313
  19.5 2.4 %join.1 = f32[32,8,128]{2,1,0:T(8,128)S(1)} custom-call(bf16[32,40,128]{2,1,0:T(8,128)(2,1)S(1)} %all_to_all.10.held), custom_call_target="tpu_custom_call" | custom-call | tf_op jit(solution)/shard_map/join/pallas_call | solution.py:314
  21.9 11.4 %all_to_all.11 = f32[32,8,128]{2,1,0:T(8,128)S(1)} all-to-all(f32[32,8,128]{2,1,0:T(8,128)S(1)} %join.1), channel_id=1, replica_groups=mesh['aa'=2,'ba'=4,'col'=4] {'aa','ba','col'}, dimensions={0} | all-to-all | bytes 262144 | tf_op jit(solution)/shard_map/all_to_all | solution.py:322
  33.3 0.7 %home.1 = bf16[8,16,128]{2,1,0:T(8,128)(2,1)} custom-call(f32[8,4,8,128]{3,2,1,0:T(8,128)S(1)} %bitcast.11, bf16[8,16,128]{2,1,0:T(8,128)(2,1)S(1)} %get-tuple-element.8.r_rows), custom_call_target="tpu_custom_call" | custom-call | tf_op jit(solution)/shard_map/home/pallas_call | solution.py:323

commit v6 on v5

--- a/solution.py
+++ b/solution.py
@@ -92,6 +92,8 @@
     ra, rb = halves(r_keys_near, r_cnt_near)
     seg = n_c * cap
     row = iota((META, LANES), 0)
+    me = (lax.axis_index("aa") * n_b + lax.axis_index("ba")) * n_c + lax.axis_index("col")
+    turn = lax.rem(me, LANES // cap) * cap
 
     def ring(vec, start):
         out = at(vec, start)
@@ -113,7 +115,7 @@
                 turned = pltpu.roll(meta, LANES - c * cap, 1) if c else meta
                 for k, vec in ((4, ra), (5, rb)):
                     turned = jnp.where(row == k, at(vec, r_at), turned)
-                turned = turned.astype(bf16)
+                turned = pltpu.roll(turned, turn, 1).astype(bf16)
                 for w in range(split_w):
                     out[(a * n_b + b) * n_c + c + w, 2 * cap : 2 * cap + META, :] = turned
     for copy in rows:
@@ -155,78 +157,77 @@
 def join_kernel(n_c, cap, split_w, srcs, held, out, s_ref, t_ref, f_ref):
     blocks = held.shape[0] // srcs
     m = srcs * cap
-    wide = f_ref.shape[1]
+    ring = LANES // cap
     rows_of = LANES // split_w
     part = cap // split_w
-    key_in = lambda shape, dim: (iota(shape, dim) % KEYS).astype(f32)
-    place = iota((cap, LANES), 1) % cap == iota((cap, LANES), 0)
-    sel = (iota((LANES, wide), 0) // cap == iota((LANES, wide), 1) // KEYS).astype(bf16)
-
-    def meta_of(i):
-        return held[pl.ds(i * srcs, srcs), 2 * cap : 2 * cap + META, :].astype(f32)
+    key = iota((KEYS, m), 0).astype(f32)
+
+    def lanes(i, bucket):
+        meta = held[pl.ds(i * srcs, srcs), 2 * cap : 2 * cap + META, :].astype(f32)
+        block = iota((META, LANES), 1) // cap
+        groups = []
+        for g in range(0, srcs, ring):
+            row = meta[g]
+            for j in range(1, ring):
+                row = jnp.where(block == (j + bucket) % ring, meta[g + j], row)
+            groups.append(row)
+        return jnp.concatenate(groups, 1)
+
+    def hot(rows, kind):
+        return rows[kind : kind + 1, :] == key
 
     def tables(i):
-        meta = meta_of(i)
-
-        def hot(kind):
-            rep = jnp.broadcast_to(meta[:, kind : kind + 1, :], (srcs, cap, LANES))
-            rep = jnp.where(place[None], rep, 0.0).astype(bf16).reshape(m, LANES)
-            return (mm(rep, sel) == key_in((m, wide), 1)).astype(bf16)
-
-        at = pl.ds(i * m, m)
+        counts, own = [], []
+        for bucket in range(n_c):
+            rows = lanes(i, bucket)
+            for k in range(2):
+                first, c = hot(rows, 2 * k).astype(bf16), hot(rows, 2 * k + 1).astype(bf16)
+                counts.append(mm_nt(first, jnp.concatenate([c, c], 0)))
+                if bucket < split_w:
+                    own.append((c, first))
+        empty = jnp.zeros((KEYS, m), bf16)
         for k, ref in enumerate((s_ref, t_ref)):
-            first, c = hot(2 * k), hot(2 * k + 1)
-            if blocks == 1:
-                f_ref[k] = mm_tn(first, c)
-            else:
-                f_ref[k] += mm_tn(first, c)
-            ref[at, 0:LANES] = c[:, 0:LANES]
-            ref[at, LANES : 2 * LANES] = first[:, 0:LANES]
-
-    def counts(k):
-        block = iota((KEYS, wide), 1) // KEYS
-        total = f_ref[k, 0:KEYS, :]
-        for j in range(1, wide // KEYS):
-            total = jnp.where(block == j, f_ref[k, j * KEYS : (j + 1) * KEYS, :], total)
-        return total
-
-    def r_hot(meta, kind):
-        row = jnp.broadcast_to(meta[:, kind : kind + 1, :], (srcs, part, LANES))
-        lane, at = iota((part, LANES), 1), iota((part, LANES), 0)
-        key = [
-            jnp.sum(jnp.where((lane == at + w * part)[None], row, 0.0), axis=2, keepdims=True)
-            for w in range(split_w)
-        ]
-        key = jnp.concatenate([x.reshape(srcs * part, 1) for x in key], 0)
-        return key == key_in((m, LANES), 1)
+            mine = own[k::2] + [(empty, empty)] * (LANES // KEYS - split_w)
+            both = [pair[0] for pair in mine] + [pair[1] for pair in mine]
+            ref[pl.ds(i * m, m), :] = jnp.concatenate(both, 0).T
+        return counts
 
     def joins(s_table, t_table, s_more, t_more, more, i):
-        meta = meta_of(i)
-        ra = r_hot(meta, 4)
-        rb = r_hot(meta, 5)
-        half = iota((m, LANES), 1) // KEYS
+        rows = lanes(i, 0)
+        ra, rb = hot(rows, 4), hot(rows, 5)
         ra16, rb16 = ra.astype(bf16), rb.astype(bf16)
-        va, vb = mm(ra16, t_table), mm(rb16, s_table)
-        pick = va[:, LANES : 2 * LANES] + va[:, 2 * LANES : 3 * LANES]
-        scale = jnp.sum(jnp.where(rb, pick, 0.0), axis=1, keepdims=True)
+        va, vb = mm_tn(t_table, ra16), mm_tn(s_table, rb16)
+        at = lambda k: va[LANES + k * KEYS : LANES + (k + 1) * KEYS]
+        scale = jnp.sum(jnp.where(rb, at(0) + at(1) + at(2), 0.0), axis=0, keepdims=True)
+        empty = jnp.zeros((KEYS, m), bf16)
 
         def sides(value, hot):
-            both = (value[:, 0:LANES], jnp.where(hot, 0.0, -BIG))
-            return [
-                jnp.concatenate([jnp.where(half == w, x, 0.0).astype(bf16) for x in both], 1)
-                for w in range(split_w)
-            ]
+            value = value.astype(bf16)
+            flag = jnp.where(hot, 0.0, -BIG).astype(bf16)
+
+            def side(w):
+                part = [empty] * (2 * LANES // KEYS)
+                part[w] = value[w * KEYS : (w + 1) * KEYS]
+                part[LANES // KEYS + w] = flag
+                return jnp.concatenate(part, 0)
+
+            return [side(w) for w in range(split_w)]
 
         def one(of_s, of_t, j, acc):
             at = pl.ds(j * m, m)
             rows = held[pl.ds(j * srcs, srcs), 0 : 2 * cap, :]
             xs, matches = [], []
             for left, ref, start in ((of_s, s_ref, 0), (of_t, t_ref, cap)):
-                x = rows[:, start : start + cap, :].reshape(m, LANES).T
+                x = rows[:, start : start + cap, :].reshape(srcs // ring, ring, cap, LANES)
+                turned = x
+                for w in range(1, split_w):
+                    shifted = jnp.concatenate([x[:, ring - w :], x[:, : ring - w]], 1)
+                    turned = jnp.where(iota(x.shape, 3) < w * rows_of, turned, shifted)
+                xs.append(turned.reshape(m, LANES).T)
                 right = ref[at]
                 for w in range(split_w):
-                    xs.append(x[w * rows_of : (w + 1) * rows_of])
-                    matches.append(jnp.maximum(mm_nt(right, left[w]), 0.0).astype(bf16))
+                    matches.append(jnp.maximum(mm(right, left[w]), 0.0).astype(bf16))
+            xs = [x[w * rows_of : (w + 1) * rows_of] for x in xs for w in range(split_w)]
             return acc + mm(jnp.concatenate(xs, 1), jnp.concatenate(matches, 0))
 
         def over(of_s, of_t, acc):
@@ -234,53 +235,59 @@
             return step(0, acc) if blocks == 1 else lax.fori_loop(0, blocks, step, acc)
 
         acc = over(sides(va, rb), sides(vb, ra), jnp.zeros((rows_of, m), f32))
-        again = lambda x: over(sides(mm(ra16, t_more), rb), sides(mm(rb16, s_more), ra), x)
-        acc = lax.cond(more, again, lambda x: x, acc)
-        size = srcs * part
-        acc = jnp.concatenate([acc[:, w * size : (w + 1) * size] for w in range(split_w)], 0).T
-        factor = scale[0:size]
+        again = lambda x: over(sides(mm_tn(t_more, ra16), rb), sides(mm_tn(s_more, rb16), ra), x)
+        acc = lax.cond(more, again, lambda x: x, acc) * scale
+        acc = jnp.concatenate([acc] * split_w, 0).T.reshape(srcs, cap, LANES)
+        result = acc[:, 0:part]
         for w in range(1, split_w):
-            factor = jnp.where(
-                iota((size, LANES), 1) < w * rows_of, factor, scale[w * size : (w + 1) * size]
-            )
-        out[pl.ds(i * srcs, srcs)] = (acc * factor).reshape(srcs, part, LANES)
-
-    def each(step):
-        if blocks == 1:
-            step(0)
-        else:
-            pl.loop(0, blocks)(step)
-
-    if blocks > 1:
+            lane = iota((srcs, part, LANES), 2)
+            result = jnp.where(lane < w * rows_of, result, acc[:, w * part : (w + 1) * part])
+        out[pl.ds(i * srcs, srcs)] = result
+
+    if blocks == 1:
+        found = tables(0)
+    else:
         f_ref[...] = jnp.zeros_like(f_ref)
-    each(tables)
-    s_counts, t_counts = counts(0), counts(1)
-    triangles = sum(mm_nt(t, s) for t in split(t_counts) for s in split(s_counts))
+
+        @pl.loop(0, blocks)
+        def _(i):
+            for k, count in enumerate(tables(i)):
+                f_ref[k] += count
+
+        found = [f_ref[k] for k in range(2 * n_c)]
+    low = iota((KEYS, LANES), 1) < KEYS
+    found += [jnp.zeros((KEYS, LANES), f32)] * (2 * (n_c % 2))
+    counts = [
+        [jnp.where(low, found[k + 2 * b], found[k + 2 * b + 2]) for b in range(0, n_c, 2)]
+        for k in range(2)
+    ]
+    s_split, t_split = [split(jnp.concatenate(x, 1)) for x in counts]
+    triangles = sum(mm_nt(t, s) for t in t_split for s in s_split)
     scale = 1.0 / jnp.sqrt(1.0 + triangles)
     hi, _ = split(scale)
     middle, rest = split(scale - hi.astype(f32))
 
     def parts(count):
-        count = count[:, 0:LANES]
         high = jnp.floor(count / EXACT) * EXACT
         return count - high, high
 
     def table(*columns):
-        x = jnp.concatenate([c.astype(f32) for c in columns], 1).astype(bf16)
-        return jnp.concatenate([x, jnp.zeros_like(x)], 0)
-
-    s_low, s_high = parts(s_counts)
-    t_low, t_high = parts(t_counts)
-    each(
-        functools.partial(
-            joins,
-            table(s_low),
-            table(t_low, hi, middle, rest, jnp.zeros((KEYS, KEYS), f32)),
-            table(s_high),
-            table(t_high),
-            jnp.maximum(jnp.max(s_high), jnp.max(t_high)) > 0.0,
-        )
+        return jnp.concatenate([c.astype(f32) for c in columns], 1).astype(bf16)
+
+    s_low, s_high = parts(counts[0][0])
+    t_low, t_high = parts(counts[1][0])
+    step = functools.partial(
+        joins,
+        table(s_low),
+        table(t_low, hi, middle, rest, jnp.zeros((KEYS, KEYS), f32)),
+        table(s_high),
+        table(t_high),
+        jnp.maximum(jnp.max(s_high), jnp.max(t_high)) > 0.0,
     )
+    if blocks == 1:
+        step(0)
+    else:
+        pl.loop(0, blocks)(step)
 
 
 def body(sizes, r_rows, r_keys, r_counts, s_rows, s_keys, s_counts, t_rows, t_keys, t_counts):
@@ -292,7 +299,6 @@
     srcs = srcs if n % srcs == 0 else n
     total_slots = n * cap
     split_w = 2 if n_c % 2 == 0 and width == LANES and cap % 16 == 0 else 1
-    wide = -(-n_c // 2) * LANES
     row = lambda x: x.reshape(1, x.shape[0])
     far = lambda x: pltpu.with_memory_space_constraint(x, pltpu.HBM)
     near = lambda x: pltpu.with_memory_space_constraint(x, pltpu.VMEM)
@@ -315,7 +321,7 @@
         functools.partial(join_kernel, n_c, cap, split_w, srcs),
         out_shape=pltpu.VMEM((n, cap // split_w, width), f32),
         scratch_shapes=[pltpu.VMEM((total_slots, 2 * LANES), bf16)] * 2
-        + [pltpu.VMEM((2, wide, wide), f32)],
+        + [pltpu.VMEM((2 * n_c, KEYS, LANES), f32)],
         compiler_params=params,
         name="join",
     )(near(held))

time: 34.2 us -> 33.9 us (level)
  no operation moved by 1% of the time
where the time goes in v6:
time: 33.9 us; the launch traced here: 33.7 us
  blocking collectives  29.6 us (87%)
  Pallas kernels  4.11 us (12%)
    all_to_all x1, blocking collectives, body(): held = lax.all_to_all(packed, AXES, split_axis=0, concat_axis=0, tiled=True)  18.2 us
    all_to_all x1, blocking collectives, body(): back = lax.all_to_all(shares, AXES, split_axis=0, concat_axis=0, tiled=True)  11.4 us
    pallas_call x1, Pallas kernels, body(): pl.pallas_call(functools.partial(join_kernel, n_c, cap, split_w, srcs), o...  2.08 us
    pallas_call x1, Pallas kernels, body(): pl.pallas_call(functools.partial(pack_kernel, n_a, n_b, n_c, cap, split_w...  1.33 us
    pallas_call x1, Pallas kernels, body(): pl.pallas_call(functools.partial(home_kernel, split_w), out_shape=jax.Sha...  0.7 us

profile of v6, /device:TPU:0, one launch (start us, length us, event | category | flops | bytes accessed | tf_op | source)
XLA Modules:
  0.0 33.7 jit_solution(13460200579123273199)
XLA Ops:
  0.0 1.3 %pack.1 = (bf16[32,40,128]{2,1,0:T(8,128)(2,1)S(1)}, bf16[8,16,128]{2,1,0:T(8,128)(2,1)S(1)}) custom-call(bf16[16,16,128]{2,1,0:T(8,128)(2,1)} %bitcast.12, bf16[8,16,128]{2,1,0:T(8,128)(2,1)} %bitcast.13, bf16[8,16,128]{2,1,0:T(8,128)(2,1)} %bitcast.14, s32[1,256]{1,0:T(1,128)} %bitcast.15, s32[1,128]{1,0:T(1,128)} %bitcast.16, s32[1,128]{1,0:T(1,128)} %bitcast.17, ...), custom_call_target="tpu_custom_call" | custom-call | tf_op jit(solution)/shard_map/pack/pallas_call | solution.py:310
  1.3 18.2 %all_to_all.10.held = bf16[32,40,128]{2,1,0:T(8,128)(2,1)S(1)} all-to-all(bf16[32,40,128]{2,1,0:T(8,128)(2,1)S(1)} %get-tuple-element.7), channel_id=1, replica_groups=mesh['aa'=2,'ba'=4,'col'=4] {'aa','ba','col'}, dimensions={0} | all-to-all | bytes 655360 | tf_op jit(solution)/shard_map/all_to_all | solution.py:319
  19.5 2.1 %join.1 = f32[32,8,128]{2,1,0:T(8,128)S(1)} custom-call(bf16[32,40,128]{2,1,0:T(8,128)(2,1)S(1)} %all_to_all.10.held), custom_call_target="tpu_custom_call" | custom-call | tf_op jit(solution)/shard_map/join/pallas_call | solution.py:320
  21.6 11.4 %all_to_all.11 = f32[32,8,128]{2,1,0:T(8,128)S(1)} all-to-all(f32[32,8,128]{2,1,0:T(8,128)S(1)} %join.1), channel_id=1, replica_groups=mesh['aa'=2,'ba'=4,'col'=4] {'aa','ba','col'}, dimensions={0} | all-to-all | bytes 262144 | tf_op jit(solution)/shard_map/all_to_all | solution.py:328
  33.0 0.7 %home.1 = bf16[8,16,128]{2,1,0:T(8,128)(2,1)} custom-call(f32[8,4,8,128]{3,2,1,0:T(8,128)S(1)} %bitcast.11, bf16[8,16,128]{2,1,0:T(8,128)(2,1)S(1)} %get-tuple-element.8.r_rows), custom_call_target="tpu_custom_call" | custom-call | tf_op jit(solution)/shard_map/home/pallas_call | solution.py:329

commit v7 on v6

--- a/solution.py
+++ b/solution.py
@@ -160,7 +160,7 @@
     ring = LANES // cap
     rows_of = LANES // split_w
     part = cap // split_w
-    key = iota((KEYS, m), 0).astype(f32)
+    key = iota((KEYS, m), 0).astype(f32).astype(bf16)
 
     def lanes(i, bucket):
         meta = held[pl.ds(i * srcs, srcs), 2 * cap : 2 * cap + META, :].astype(f32)
@@ -174,44 +174,39 @@
         return jnp.concatenate(groups, 1)
 
     def hot(rows, kind):
-        return rows[kind : kind + 1, :] == key
+        return jnp.broadcast_to(rows[kind : kind + 1, :], (KEYS, m)).astype(bf16) == key
+
+    def one_hot(rows, kind):
+        return jnp.where(hot(rows, kind), jnp.ones_like(key), jnp.zeros_like(key))
 
     def tables(i):
         counts, own = [], []
         for bucket in range(n_c):
             rows = lanes(i, bucket)
             for k in range(2):
-                first, c = hot(rows, 2 * k).astype(bf16), hot(rows, 2 * k + 1).astype(bf16)
+                first, c = one_hot(rows, 2 * k), one_hot(rows, 2 * k + 1)
                 counts.append(mm_nt(first, jnp.concatenate([c, c], 0)))
                 if bucket < split_w:
                     own.append((c, first))
-        empty = jnp.zeros((KEYS, m), bf16)
         for k, ref in enumerate((s_ref, t_ref)):
-            mine = own[k::2] + [(empty, empty)] * (LANES // KEYS - split_w)
-            both = [pair[0] for pair in mine] + [pair[1] for pair in mine]
-            ref[pl.ds(i * m, m), :] = jnp.concatenate(both, 0).T
+            for w, pair in enumerate(own[k::2]):
+                ref[w, pl.ds(i * m, m), :] = jnp.concatenate(pair, 0).T
         return counts
 
     def joins(s_table, t_table, s_more, t_more, more, i):
         rows = lanes(i, 0)
         ra, rb = hot(rows, 4), hot(rows, 5)
-        ra16, rb16 = ra.astype(bf16), rb.astype(bf16)
+        ra16, rb16 = one_hot(rows, 4), one_hot(rows, 5)
         va, vb = mm_tn(t_table, ra16), mm_tn(s_table, rb16)
         at = lambda k: va[LANES + k * KEYS : LANES + (k + 1) * KEYS]
-        scale = jnp.sum(jnp.where(rb, at(0) + at(1) + at(2), 0.0), axis=0, keepdims=True)
-        empty = jnp.zeros((KEYS, m), bf16)
+        scale = jnp.sum(jnp.where(rb16 > 0.5, at(0) + at(1) + at(2), 0.0), axis=0, keepdims=True)
 
         def sides(value, hot):
             value = value.astype(bf16)
-            flag = jnp.where(hot, 0.0, -BIG).astype(bf16)
-
-            def side(w):
-                part = [empty] * (2 * LANES // KEYS)
-                part[w] = value[w * KEYS : (w + 1) * KEYS]
-                part[LANES // KEYS + w] = flag
-                return jnp.concatenate(part, 0)
-
-            return [side(w) for w in range(split_w)]
+            flag = jnp.where(hot, jnp.zeros_like(key), jnp.full_like(key, -BIG))
+            return [
+                jnp.concatenate([value[w * KEYS : (w + 1) * KEYS], flag], 0) for w in range(split_w)
+            ]
 
         def one(of_s, of_t, j, acc):
             at = pl.ds(j * m, m)
@@ -224,9 +219,8 @@
                     shifted = jnp.concatenate([x[:, ring - w :], x[:, : ring - w]], 1)
                     turned = jnp.where(iota(x.shape, 3) < w * rows_of, turned, shifted)
                 xs.append(turned.reshape(m, LANES).T)
-                right = ref[at]
                 for w in range(split_w):
-                    matches.append(jnp.maximum(mm(right, left[w]), 0.0).astype(bf16))
+                    matches.append(jnp.maximum(mm(ref[w, at], left[w]), 0.0).astype(bf16))
             xs = [x[w * rows_of : (w + 1) * rows_of] for x in xs for w in range(split_w)]
             return acc + mm(jnp.concatenate(xs, 1), jnp.concatenate(matches, 0))
 
@@ -320,7 +314,7 @@
     shares = pl.pallas_call(
         functools.partial(join_kernel, n_c, cap, split_w, srcs),
         out_shape=pltpu.VMEM((n, cap // split_w, width), f32),
-        scratch_shapes=[pltpu.VMEM((total_slots, 2 * LANES), bf16)] * 2
+        scratch_shapes=[pltpu.VMEM((split_w, total_slots, LANES), bf16)] * 2
         + [pltpu.VMEM((2 * n_c, KEYS, LANES), f32)],
         compiler_params=params,
         name="join",

time: 33.9 us -> 33.9 us (level)
  no operation moved by 1% of the time
where the time goes in v7:
time: 33.9 us; the launch traced here: 33.7 us
  blocking collectives  29.6 us (87%)
  Pallas kernels  4.12 us (12%)
    all_to_all x1, blocking collectives, body(): held = lax.all_to_all(packed, AXES, split_axis=0, concat_axis=0, tiled=True)  18.2 us
    all_to_all x1, blocking collectives, body(): back = lax.all_to_all(shares, AXES, split_axis=0, concat_axis=0, tiled=True)  11.4 us
    pallas_call x1, Pallas kernels, body(): pl.pallas_call(functools.partial(join_kernel, n_c, cap, split_w, srcs), o...  2.09 us
    pallas_call x1, Pallas kernels, body(): pl.pallas_call(functools.partial(pack_kernel, n_a, n_b, n_c, cap, split_w...  1.33 us
    pallas_call x1, Pallas kernels, body(): pl.pallas_call(functools.partial(home_kernel, split_w), out_shape=jax.Sha...  0.7 us

profile of v7, /device:TPU:0, one launch (start us, length us, event | category | flops | bytes accessed | tf_op | source)
XLA Modules:
  0.0 33.7 jit_solution(10081009274963120309)
XLA Ops:
  0.0 1.3 %pack.1 = (bf16[32,40,128]{2,1,0:T(8,128)(2,1)S(1)}, bf16[8,16,128]{2,1,0:T(8,128)(2,1)S(1)}) custom-call(bf16[16,16,128]{2,1,0:T(8,128)(2,1)} %bitcast.12, bf16[8,16,128]{2,1,0:T(8,128)(2,1)} %bitcast.13, bf16[8,16,128]{2,1,0:T(8,128)(2,1)} %bitcast.14, s32[1,256]{1,0:T(1,128)} %bitcast.15, s32[1,128]{1,0:T(1,128)} %bitcast.16, s32[1,128]{1,0:T(1,128)} %bitcast.17, ...), custom_call_target="tpu_custom_call" | custom-call | tf_op jit(solution)/shard_map/pack/pallas_call | solution.py:304
  1.3 18.2 %all_to_all.10.held = bf16[32,40,128]{2,1,0:T(8,128)(2,1)S(1)} all-to-all(bf16[32,40,128]{2,1,0:T(8,128)(2,1)S(1)} %get-tuple-element.7), channel_id=1, replica_groups=mesh['aa'=2,'ba'=4,'col'=4] {'aa','ba','col'}, dimensions={0} | all-to-all | bytes 655360 | tf_op jit(solution)/shard_map/all_to_all | solution.py:313
  19.5 2.1 %join.1 = f32[32,8,128]{2,1,0:T(8,128)S(1)} custom-call(bf16[32,40,128]{2,1,0:T(8,128)(2,1)S(1)} %all_to_all.10.held), custom_call_target="tpu_custom_call" | custom-call | tf_op jit(solution)/shard_map/join/pallas_call | solution.py:314
  21.6 11.4 %all_to_all.11 = f32[32,8,128]{2,1,0:T(8,128)S(1)} all-to-all(f32[32,8,128]{2,1,0:T(8,128)S(1)} %join.1), channel_id=1, replica_groups=mesh['aa'=2,'ba'=4,'col'=4] {'aa','ba','col'}, dimensions={0} | all-to-all | bytes 262144 | tf_op jit(solution)/shard_map/all_to_all | solution.py:322
  33.0 0.7 %home.1 = bf16[8,16,128]{2,1,0:T(8,128)(2,1)} custom-call(f32[8,4,8,128]{3,2,1,0:T(8,128)S(1)} %bitcast.11, bf16[8,16,128]{2,1,0:T(8,128)(2,1)S(1)} %get-tuple-element.8.r_rows), custom_call_target="tpu_custom_call" | custom-call | tf_op jit(solution)/shard_map/home/pallas_call | solution.py:323

commit v8 on v7

--- a/solution.py
+++ b/solution.py
@@ -154,7 +154,7 @@
 EXACT = 256.0
 
 
-def join_kernel(n_c, cap, split_w, srcs, held, out, s_ref, t_ref, f_ref):
+def join_kernel(n_c, cap, split_w, srcs, held, out, s_ref, t_ref, own_ref, all_ref):
     blocks = held.shape[0] // srcs
     m = srcs * cap
     ring = LANES // cap
@@ -173,42 +173,69 @@
             groups.append(row)
         return jnp.concatenate(groups, 1)
 
-    def hot(rows, kind):
+    def hot_of(rows, kind):
         return jnp.broadcast_to(rows[kind : kind + 1, :], (KEYS, m)).astype(bf16) == key
 
     def one_hot(rows, kind):
-        return jnp.where(hot(rows, kind), jnp.ones_like(key), jnp.zeros_like(key))
-
-    def tables(i):
-        counts, own = [], []
-        for bucket in range(n_c):
-            rows = lanes(i, bucket)
-            for k in range(2):
-                first, c = one_hot(rows, 2 * k), one_hot(rows, 2 * k + 1)
-                counts.append(mm_nt(first, jnp.concatenate([c, c], 0)))
-                if bucket < split_w:
-                    own.append((c, first))
+        return jnp.where(hot_of(rows, kind), jnp.ones_like(key), jnp.zeros_like(key))
+
+    def stack(i, kind, buckets):
+        return jnp.concatenate([one_hot(lanes(i, bucket), kind) for bucket in buckets], 0)
+
+    own = range(split_w)
+
+    def own_counts(i):
+        counts = []
         for k, ref in enumerate((s_ref, t_ref)):
-            for w, pair in enumerate(own[k::2]):
-                ref[w, pl.ds(i * m, m), :] = jnp.concatenate(pair, 0).T
+            first, c = stack(i, 2 * k, own), stack(i, 2 * k + 1, own)
+            counts.append(mm_nt(c, first))
+            for w in own:
+                at = slice(w * KEYS, (w + 1) * KEYS)
+                ref[w, pl.ds(i * m, m), :] = jnp.concatenate([c[at], first[at]], 0).T
         return counts
 
-    def joins(s_table, t_table, s_more, t_more, more, i):
+    def all_counts(i):
+        every = range(n_c)
+        return [mm_nt(stack(i, 2 * k, every), stack(i, 2 * k + 1, every)) for k in range(2)]
+
+    def tables(own_found):
+        found = []
+        for count in own_found:
+            same = iota(count.shape, 0) // KEYS == iota(count.shape, 1) // KEYS
+            count = jnp.where(same, count, 0.0)
+            high = jnp.floor(count / EXACT) * EXACT
+            found.append((count - high, high))
+        more = jnp.maximum(jnp.max(found[0][1]), jnp.max(found[1][1])) > 0.0
+        return [(low.astype(bf16), high.astype(bf16)) for low, high in found], more
+
+    def halves_of(all_found):
+        halves = []
+        for count in all_found:
+            block = iota((KEYS, count.shape[1]), 1) // KEYS
+            total = count[0:KEYS]
+            for b in range(1, n_c):
+                total = jnp.where(block == b, count[b * KEYS : (b + 1) * KEYS], total)
+            halves.append(split(total))
+        return halves
+
+    def scales(halves):
+        triangles = sum(mm_nt(s, t) for s in halves[0] for t in halves[1])
+        scale = 1.0 / jnp.sqrt(1.0 + triangles)
+        hi, _ = split(scale)
+        middle, rest = split(scale - hi.astype(f32))
+        return jnp.concatenate([hi, middle, rest], 0)
+
+    def joins(i, found, more, between=()):
         rows = lanes(i, 0)
-        ra, rb = hot(rows, 4), hot(rows, 5)
-        ra16, rb16 = one_hot(rows, 4), one_hot(rows, 5)
-        va, vb = mm_tn(t_table, ra16), mm_tn(s_table, rb16)
-        at = lambda k: va[LANES + k * KEYS : LANES + (k + 1) * KEYS]
-        scale = jnp.sum(jnp.where(rb16 > 0.5, at(0) + at(1) + at(2), 0.0), axis=0, keepdims=True)
-
-        def sides(value, hot):
-            value = value.astype(bf16)
-            flag = jnp.where(hot, jnp.zeros_like(key), jnp.full_like(key, -BIG))
-            return [
-                jnp.concatenate([value[w * KEYS : (w + 1) * KEYS], flag], 0) for w in range(split_w)
-            ]
-
-        def one(of_s, of_t, j, acc):
+        ra, rb = [jnp.concatenate([one_hot(rows, k)] * split_w, 0) for k in (4, 5)]
+        (s_low, s_high), (t_low, t_high) = found
+
+        def sides(table, hot, kind_flag):
+            value = mm(table, hot).astype(bf16)
+            flag = jnp.where(hot_of(rows, kind_flag), jnp.zeros_like(key), jnp.full_like(key, -BIG))
+            return [jnp.concatenate([value[w * KEYS : (w + 1) * KEYS], flag], 0) for w in own]
+
+        def one(of_s, of_t, between, j, acc):
             at = pl.ds(j * m, m)
             rows = held[pl.ds(j * srcs, srcs), 0 : 2 * cap, :]
             xs, matches = [], []
@@ -219,18 +246,29 @@
                     shifted = jnp.concatenate([x[:, ring - w :], x[:, : ring - w]], 1)
                     turned = jnp.where(iota(x.shape, 3) < w * rows_of, turned, shifted)
                 xs.append(turned.reshape(m, LANES).T)
-                for w in range(split_w):
+                for w in own:
+                    if len(matches) in between:
+                        between[len(matches)]()
                     matches.append(jnp.maximum(mm(ref[w, at], left[w]), 0.0).astype(bf16))
-            xs = [x[w * rows_of : (w + 1) * rows_of] for x in xs for w in range(split_w)]
+            xs = [x[w * rows_of : (w + 1) * rows_of] for x in xs for w in own]
             return acc + mm(jnp.concatenate(xs, 1), jnp.concatenate(matches, 0))
 
-        def over(of_s, of_t, acc):
-            step = functools.partial(one, of_s, of_t)
+        def over(of_s, of_t, acc, between=()):
+            step = functools.partial(one, of_s, of_t, between)
             return step(0, acc) if blocks == 1 else lax.fori_loop(0, blocks, step, acc)
 
-        acc = over(sides(va, rb), sides(vb, ra), jnp.zeros((rows_of, m), f32))
-        again = lambda x: over(sides(mm_tn(t_more, ra16), rb), sides(mm_tn(s_more, rb16), ra), x)
-        acc = lax.cond(more, again, lambda x: x, acc) * scale
+        acc = over(sides(t_low, ra, 5), sides(s_low, rb, 4), jnp.zeros((rows_of, m), f32), between)
+        again = lambda x: over(sides(t_high, ra, 5), sides(s_high, rb, 4), x)
+        return acc, lambda x: lax.cond(more, again, lambda x: x, x)
+
+    def factor(i, table):
+        rows = lanes(i, 0)
+        at = mm(table, one_hot(rows, 4))
+        at = at[0:KEYS] + at[KEYS : 2 * KEYS] + at[2 * KEYS : 3 * KEYS]
+        return jnp.sum(jnp.where(one_hot(rows, 5) > 0.5, at, 0.0), axis=0, keepdims=True)
+
+    def finish(i, acc, by):
+        acc = acc * by
         acc = jnp.concatenate([acc] * split_w, 0).T.reshape(srcs, cap, LANES)
         result = acc[:, 0:part]
         for w in range(1, split_w):
@@ -239,49 +277,33 @@
         out[pl.ds(i * srcs, srcs)] = result
 
     if blocks == 1:
-        found = tables(0)
-    else:
-        f_ref[...] = jnp.zeros_like(f_ref)
-
-        @pl.loop(0, blocks)
-        def _(i):
-            for k, count in enumerate(tables(i)):
-                f_ref[k] += count
-
-        found = [f_ref[k] for k in range(2 * n_c)]
-    low = iota((KEYS, LANES), 1) < KEYS
-    found += [jnp.zeros((KEYS, LANES), f32)] * (2 * (n_c % 2))
-    counts = [
-        [jnp.where(low, found[k + 2 * b], found[k + 2 * b + 2]) for b in range(0, n_c, 2)]
-        for k in range(2)
-    ]
-    s_split, t_split = [split(jnp.concatenate(x, 1)) for x in counts]
-    triangles = sum(mm_nt(t, s) for t in t_split for s in s_split)
-    scale = 1.0 / jnp.sqrt(1.0 + triangles)
-    hi, _ = split(scale)
-    middle, rest = split(scale - hi.astype(f32))
-
-    def parts(count):
-        high = jnp.floor(count / EXACT) * EXACT
-        return count - high, high
-
-    def table(*columns):
-        return jnp.concatenate([c.astype(f32) for c in columns], 1).astype(bf16)
-
-    s_low, s_high = parts(counts[0][0])
-    t_low, t_high = parts(counts[1][0])
-    step = functools.partial(
-        joins,
-        table(s_low),
-        table(t_low, hi, middle, rest, jnp.zeros((KEYS, KEYS), f32)),
-        table(s_high),
-        table(t_high),
-        jnp.maximum(jnp.max(s_high), jnp.max(t_high)) > 0.0,
-    )
-    if blocks == 1:
-        step(0)
-    else:
-        pl.loop(0, blocks)(step)
+        kept = {}
+        found = tables(own_counts(0))
+        halves = halves_of(all_counts(0))
+        between = {
+            0: lambda: kept.update(table=scales(halves)),
+            split_w: lambda: kept.update(by=factor(0, kept["table"])),
+        }
+        acc, rest = joins(0, *found, between)
+        finish(0, rest(acc), kept["by"])
+        return
+
+    own_ref[...] = jnp.zeros_like(own_ref)
+    all_ref[...] = jnp.zeros_like(all_ref)
+
+    @pl.loop(0, blocks)
+    def _(i):
+        for k, (mine, every) in enumerate(zip(own_counts(i), all_counts(i))):
+            own_ref[k] += mine
+            all_ref[k] += every
+
+    found, more = tables([own_ref[0], own_ref[1]])
+    table = scales(halves_of([all_ref[0], all_ref[1]]))
+
+    @pl.loop(0, blocks)
+    def _(i):
+        acc, rest = joins(i, found, more)
+        finish(i, rest(acc), factor(i, table))
 
 
 def body(sizes, r_rows, r_keys, r_counts, s_rows, s_keys, s_counts, t_rows, t_keys, t_counts):
@@ -315,7 +337,10 @@
         functools.partial(join_kernel, n_c, cap, split_w, srcs),
         out_shape=pltpu.VMEM((n, cap // split_w, width), f32),
         scratch_shapes=[pltpu.VMEM((split_w, total_slots, LANES), bf16)] * 2
-        + [pltpu.VMEM((2 * n_c, KEYS, LANES), f32)],
+        + [
+            pltpu.VMEM((2, split_w * KEYS, split_w * KEYS), f32),
+            pltpu.VMEM((2, n_c * KEYS, n_c * KEYS), f32),
+        ],
         compiler_params=params,
         name="join",
     )(near(held))

time: 33.9 us -> 33.5 us (0.988)
  Pallas kernels: 4.12 us -> 3.75 us
    pallas_call x1, Pallas kernels: 2.09 us -> 1.72 us  [body(): pl.pallas_call(functools.partial(join_kernel, n_c, cap, split_w, srcs), o...]
where the time goes in v8:
time: 33.5 us; the launch traced here: 33.4 us
  blocking collectives  29.6 us (88%)
  Pallas kernels  3.75 us (11%)
    all_to_all x1, blocking collectives, body(): held = lax.all_to_all(packed, AXES, split_axis=0, concat_axis=0, tiled=True)  18.2 us
    all_to_all x1, blocking collectives, body(): back = lax.all_to_all(shares, AXES, split_axis=0, concat_axis=0, tiled=True)  11.4 us
    pallas_call x1, Pallas kernels, body(): pl.pallas_call(functools.partial(join_kernel, n_c, cap, split_w, srcs), o...  1.72 us
    pallas_call x1, Pallas kernels, body(): pl.pallas_call(functools.partial(pack_kernel, n_a, n_b, n_c, cap, split_w...  1.33 us
    pallas_call x1, Pallas kernels, body(): pl.pallas_call(functools.partial(home_kernel, split_w), out_shape=jax.Sha...  0.7 us

profile of v8, /device:TPU:0, one launch (start us, length us, event | category | flops | bytes accessed | tf_op | source)
XLA Modules:
  0.0 33.4 jit_solution(3660302192505698711)
XLA Ops:
  0.0 1.3 %pack.1 = (bf16[32,40,128]{2,1,0:T(8,128)(2,1)S(1)}, bf16[8,16,128]{2,1,0:T(8,128)(2,1)S(1)}) custom-call(bf16[16,16,128]{2,1,0:T(8,128)(2,1)} %bitcast.12, bf16[8,16,128]{2,1,0:T(8,128)(2,1)} %bitcast.13, bf16[8,16,128]{2,1,0:T(8,128)(2,1)} %bitcast.14, s32[1,256]{1,0:T(1,128)} %bitcast.15, s32[1,128]{1,0:T(1,128)} %bitcast.16, s32[1,128]{1,0:T(1,128)} %bitcast.17, ...), custom_call_target="tpu_custom_call" | custom-call | tf_op jit(solution)/shard_map/pack/pallas_call | solution.py:326
  1.3 18.2 %all_to_all.10.held = bf16[32,40,128]{2,1,0:T(8,128)(2,1)S(1)} all-to-all(bf16[32,40,128]{2,1,0:T(8,128)(2,1)S(1)} %get-tuple-element.7), channel_id=1, replica_groups=mesh['aa'=2,'ba'=4,'col'=4] {'aa','ba','col'}, dimensions={0} | all-to-all | bytes 655360 | tf_op jit(solution)/shard_map/all_to_all | solution.py:335
  19.5 1.7 %join.1 = f32[32,8,128]{2,1,0:T(8,128)S(1)} custom-call(bf16[32,40,128]{2,1,0:T(8,128)(2,1)S(1)} %all_to_all.10.held), custom_call_target="tpu_custom_call" | custom-call | tf_op jit(solution)/shard_map/join/pallas_call | solution.py:336
  21.3 11.4 %all_to_all.11 = f32[32,8,128]{2,1,0:T(8,128)S(1)} all-to-all(f32[32,8,128]{2,1,0:T(8,128)S(1)} %join.1), channel_id=1, replica_groups=mesh['aa'=2,'ba'=4,'col'=4] {'aa','ba','col'}, dimensions={0} | all-to-all | bytes 262144 | tf_op jit(solution)/shard_map/all_to_all | solution.py:347
  32.6 0.7 %home.1 = bf16[8,16,128]{2,1,0:T(8,128)(2,1)} custom-call(f32[8,4,8,128]{3,2,1,0:T(8,128)S(1)} %bitcast.11, bf16[8,16,128]{2,1,0:T(8,128)(2,1)S(1)} %get-tuple-element.8.r_rows), custom_call_target="tpu_custom_call" | custom-call | tf_op jit(solution)/shard_map/home/pallas_call | solution.py:348

commit v9 on v8

--- a/solution.py
+++ b/solution.py
@@ -9,7 +9,7 @@
 
 KEYS = 64
 LANES = 128
-META = 8
+TILE = 4
 AXES = ("aa", "ba", "col")
 f32 = jnp.float32
 bf16 = jnp.bfloat16
@@ -91,33 +91,54 @@
     ta, tc = halves(t_keys_near, t_cnt_near)
     ra, rb = halves(r_keys_near, r_cnt_near)
     seg = n_c * cap
-    row = iota((META, LANES), 0)
+    tiles = out.shape[0] // (n_a * n_b * n_c)
+    meta_rows = tiles * TILE - 2 * cap
+    row = iota((meta_rows, LANES), 0)
+    lane = iota((1, LANES), 1)
     me = (lax.axis_index("aa") * n_b + lax.axis_index("ba")) * n_c + lax.axis_index("col")
-    turn = lax.rem(me, LANES // cap) * cap
-
-    def ring(vec, start):
-        out = at(vec, start)
-        size = seg
-        while size < LANES:
-            out = jnp.where(iota((1, LANES), 1) < size, out, pltpu.roll(out, size, 1))
-            size *= 2
-        return out
-
-    s_meta = [(ring(sb, b * seg), ring(sc, b * seg)) for b in range(n_b)]
-    t_meta = [(ring(ta, a * seg), ring(tc, a * seg)) for a in range(n_a)]
+    turn = lax.rem(me, n_c) * cap
+
+    def put(d, start, value):
+        for t in range(value.shape[0] // TILE):
+            out[d * tiles + start // TILE + t] = value[t * TILE : (t + 1) * TILE]
+
+    def pairs(first, second, start):
+        first, second = at(first, start), at(second, start)
+        if seg == LANES:
+            return [first, second]
+        return [jnp.where(lane < seg, first, pltpu.roll(second, seg, 1))]
+
+    def repeated(first, second):
+        slots = first.shape[1]
+        groups = slots // cap
+        mine = iota((groups, slots), 1) // cap == iota((groups, slots), 0)
+        same = iota((slots, LANES), 0) % cap == iota((slots, LANES), 1) % cap
+        low = iota((slots, LANES), 1) < seg
+        spread = lambda x, to: mm(jnp.where(mine, x, 0.0).astype(bf16), to.astype(bf16))
+        if seg == LANES:
+            return [spread(first, same), spread(second, same)]
+        return [spread(first, same & low) + spread(second, same & ~low)]
+
+    def turned(meta, by):
+        if seg == LANES:
+            return pltpu.roll(meta, by, 1)
+        return jnp.where(
+            iota(meta.shape, 1) % seg >= by, pltpu.roll(meta, by, 1), pltpu.roll(meta, by + seg, 1)
+        )
+
+    s_meta = [pairs(sb, sc, b * seg) for b in range(n_b)]
+    t_meta = [pairs(ta, tc, a * seg) for a in range(n_a)]
+    r_meta = repeated(ra, rb)
     for a in range(n_a):
         for b in range(n_b):
-            meta = jnp.zeros((META, LANES), f32)
-            for k, value in enumerate(s_meta[b] + t_meta[a]):
+            g = a * n_b + b
+            meta = jnp.zeros((meta_rows, LANES), f32)
+            for k, value in enumerate(s_meta[b] + t_meta[a] + [x[g : g + 1] for x in r_meta]):
                 meta = jnp.where(row == k, value, meta)
-            r_at = (a * n_b + b) * cap
             for c in range(0, n_c, split_w):
-                turned = pltpu.roll(meta, LANES - c * cap, 1) if c else meta
-                for k, vec in ((4, ra), (5, rb)):
-                    turned = jnp.where(row == k, at(vec, r_at), turned)
-                turned = pltpu.roll(turned, turn, 1).astype(bf16)
+                part = turned(meta, lax.rem(turn + seg - c * cap, seg)).astype(bf16)
                 for w in range(split_w):
-                    out[(a * n_b + b) * n_c + c + w, 2 * cap : 2 * cap + META, :] = turned
+                    put(g * n_c + c + w, 2 * cap, part)
     for copy in rows:
         copy.wait()
 
@@ -131,11 +152,11 @@
         for b in range(n_b):
             for w, part in enumerate(parts(s_near, b * n_c + c)):
                 for a in range(n_a):
-                    out[(a * n_b + b) * n_c + c + w, 0:cap, :] = part
+                    put((a * n_b + b) * n_c + c + w, 0, part)
         for a in range(n_a):
             for w, part in enumerate(parts(t_near, a * n_c + c)):
                 for b in range(n_b):
-                    out[(a * n_b + b) * n_c + c + w, cap : 2 * cap, :] = part
+                    put((a * n_b + b) * n_c + c + w, cap, part)
 
 
 def home_kernel(split_w, shares, r_rows, out):
@@ -154,27 +175,40 @@
 EXACT = 256.0
 
 
-def join_kernel(n_c, cap, split_w, srcs, held, out, s_ref, t_ref, own_ref, all_ref):
-    blocks = held.shape[0] // srcs
+def join_kernel(n_c, cap, split_w, srcs, tiles, held, out, s_ref, t_ref, own_ref, all_ref):
+    blocks = held.shape[0] // (srcs * tiles)
     m = srcs * cap
-    ring = LANES // cap
+    seg = n_c * cap
     rows_of = LANES // split_w
     part = cap // split_w
     key = iota((KEYS, m), 0).astype(f32).astype(bf16)
 
+    def block_of(i):
+        return held[pl.ds(i * srcs * tiles, srcs * tiles)].reshape(srcs, tiles, TILE, LANES)
+
     def lanes(i, bucket):
-        meta = held[pl.ds(i * srcs, srcs), 2 * cap : 2 * cap + META, :].astype(f32)
-        block = iota((META, LANES), 1) // cap
+        meta = block_of(i)[:, 2 * cap // TILE :].astype(f32)
+        meta = meta.reshape(srcs, meta.shape[1] * TILE, LANES)
+        block = iota(meta.shape[1:], 1) % seg // cap
         groups = []
-        for g in range(0, srcs, ring):
+        for g in range(0, srcs, n_c):
             row = meta[g]
-            for j in range(1, ring):
-                row = jnp.where(block == (j + bucket) % ring, meta[g + j], row)
+            for j in range(1, n_c):
+                row = jnp.where(block == (j + bucket) % n_c, meta[g + j], row)
             groups.append(row)
-        return jnp.concatenate(groups, 1)
+        if seg == LANES:
+            rows = jnp.concatenate(groups, 1)
+            return [rows[k : k + 1] for k in range(6)]
+        low = iota(meta.shape[1:], 1) < seg
+        swapped = [
+            (jnp.where(low, x, pltpu.roll(y, seg, 1)), jnp.where(low, pltpu.roll(x, seg, 1), y))
+            for x, y in zip(groups[0::2], groups[1::2])
+        ]
+        both = [jnp.concatenate(x, 1) for x in zip(*swapped)]
+        return [both[k % 2][k // 2 : k // 2 + 1] for k in range(6)]
 
     def hot_of(rows, kind):
-        return jnp.broadcast_to(rows[kind : kind + 1, :], (KEYS, m)).astype(bf16) == key
+        return jnp.broadcast_to(rows[kind], (KEYS, m)).astype(bf16) == key
 
     def one_hot(rows, kind):
         return jnp.where(hot_of(rows, kind), jnp.ones_like(key), jnp.zeros_like(key))
@@ -237,15 +271,16 @@
 
         def one(of_s, of_t, between, j, acc):
             at = pl.ds(j * m, m)
-            rows = held[pl.ds(j * srcs, srcs), 0 : 2 * cap, :]
+            rows = block_of(j)
             xs, matches = [], []
             for left, ref, start in ((of_s, s_ref, 0), (of_t, t_ref, cap)):
-                x = rows[:, start : start + cap, :].reshape(srcs // ring, ring, cap, LANES)
-                turned = x
+                x = rows[:, start // TILE : (start + cap) // TILE]
+                x = x.reshape(srcs // n_c, n_c, cap, LANES)
+                turned = x.reshape(m, LANES)
                 for w in range(1, split_w):
-                    shifted = jnp.concatenate([x[:, ring - w :], x[:, : ring - w]], 1)
-                    turned = jnp.where(iota(x.shape, 3) < w * rows_of, turned, shifted)
-                xs.append(turned.reshape(m, LANES).T)
+                    shifted = jnp.concatenate([x[:, n_c - w :], x[:, : n_c - w]], 1).reshape(m, LANES)
+                    turned = jnp.concatenate([turned[:, : w * rows_of], shifted[:, w * rows_of :]], 1)
+                xs.append(turned.T)
                 for w in own:
                     if len(matches) in between:
                         between[len(matches)]()
@@ -315,6 +350,9 @@
     srcs = srcs if n % srcs == 0 else n
     total_slots = n * cap
     split_w = 2 if n_c % 2 == 0 and width == LANES and cap % 16 == 0 else 1
+    meta_rows = 8 if n_c * cap == LANES else 4
+    assert n_c * cap in (LANES, LANES // 2) and n % (2 * n_c) == 0 and n * cap < BIG
+    tiles = (2 * cap + meta_rows) // TILE
     row = lambda x: x.reshape(1, x.shape[0])
     far = lambda x: pltpu.with_memory_space_constraint(x, pltpu.HBM)
     near = lambda x: pltpu.with_memory_space_constraint(x, pltpu.VMEM)
@@ -326,7 +364,7 @@
     packed, r_kept = pl.pallas_call(
         functools.partial(pack_kernel, n_a, n_b, n_c, cap, split_w),
         in_specs=[pl.BlockSpec(memory_space=pltpu.HBM)] * 9,
-        out_shape=(pltpu.VMEM((n, 2 * cap + META, width), bf16), near_like(blocked[2])),
+        out_shape=(pltpu.VMEM((n * tiles, TILE, width), bf16), near_like(blocked[2])),
         scratch_shapes=[near_like(x) for x in (*blocked[:2], *small)]
         + [pltpu.SemaphoreType.DMA((9,))],
         compiler_params=params,
@@ -334,7 +372,7 @@
     )(*map(far, (*blocked, *small)))
     held = lax.all_to_all(packed, AXES, split_axis=0, concat_axis=0, tiled=True)
     shares = pl.pallas_call(
-        functools.partial(join_kernel, n_c, cap, split_w, srcs),
+        functools.partial(join_kernel, n_c, cap, split_w, srcs, tiles),
         out_shape=pltpu.VMEM((n, cap // split_w, width), f32),
         scratch_shapes=[pltpu.VMEM((split_w, total_slots, LANES), bf16)] * 2
         + [

time: 33.5 us -> 32.9 us (0.982)
  blocking collectives: 29.6 us -> 28.9 us
    all_to_all x1, blocking collectives: 18.2 us -> 17.8 us  [body(): held = lax.all_to_all(packed, AXES, split_axis=0, concat_axis=0, tiled=True)]
where the time goes in v9:
time: 32.9 us; the launch traced here: 32.7 us
  blocking collectives  28.9 us (88%)
  Pallas kernels  3.81 us (12%)
    all_to_all x1, blocking collectives, body(): held = lax.all_to_all(packed, AXES, split_axis=0, concat_axis=0, tiled=True)  17.8 us
    all_to_all x1, blocking collectives, body(): back = lax.all_to_all(shares, AXES, split_axis=0, concat_axis=0, tiled=True)  11.1 us
    pallas_call x1, Pallas kernels, body(): pl.pallas_call(functools.partial(join_kernel, n_c, cap, split_w, srcs, ti...  1.8 us
    pallas_call x1, Pallas kernels, body(): pl.pallas_call(functools.partial(pack_kernel, n_a, n_b, n_c, cap, split_w...  1.3 us
    pallas_call x1, Pallas kernels, body(): pl.pallas_call(functools.partial(home_kernel, split_w), out_shape=jax.Sha...  0.7 us

profile of v9, /device:TPU:0, one launch (start us, length us, event | category | flops | bytes accessed | tf_op | source)
XLA Modules:
  0.0 32.7 jit_solution(11132182554593923863)
XLA Ops:
  0.0 1.3 %pack.1 = (bf16[288,4,128]{2,1,0:T(4,128)(2,1)S(1)}, bf16[8,16,128]{2,1,0:T(8,128)(2,1)S(1)}) custom-call(bf16[16,16,128]{2,1,0:T(8,128)(2,1)} %bitcast.12, bf16[8,16,128]{2,1,0:T(8,128)(2,1)} %bitcast.13, bf16[8,16,128]{2,1,0:T(8,128)(2,1)} %bitcast.14, s32[1,256]{1,0:T(1,128)} %bitcast.15, s32[1,128]{1,0:T(1,128)} %bitcast.16, s32[1,128]{1,0:T(1,128)} %bitcast.17, ...), custom_call_target="tpu_custom_call" | custom-call | tf_op jit(solution)/shard_map/pack/pallas_call | solution.py:364
  1.3 17.8 %all_to_all.10.held = bf16[288,4,128]{2,1,0:T(4,128)(2,1)S(1)} all-to-all(bf16[288,4,128]{2,1,0:T(4,128)(2,1)S(1)} %get-tuple-element.7), channel_id=1, replica_groups=mesh['aa'=2,'ba'=4,'col'=4] {'aa','ba','col'}, dimensions={0} | all-to-all | bytes 589824 | tf_op jit(solution)/shard_map/all_to_all | solution.py:373
  19.1 1.8 %join.1 = f32[32,8,128]{2,1,0:T(8,128)S(1)} custom-call(bf16[288,4,128]{2,1,0:T(4,128)(2,1)S(1)} %all_to_all.10.held), custom_call_target="tpu_custom_call" | custom-call | tf_op jit(solution)/shard_map/join/pallas_call | solution.py:374
  20.9 11.1 %all_to_all.11 = f32[32,8,128]{2,1,0:T(8,128)S(1)} all-to-all(f32[32,8,128]{2,1,0:T(8,128)S(1)} %join.1), channel_id=1, replica_groups=mesh['aa'=2,'ba'=4,'col'=4] {'aa','ba','col'}, dimensions={0} | all-to-all | bytes 262144 | tf_op jit(solution)/shard_map/all_to_all | solution.py:385
  32.0 0.7 %home.1 = bf16[8,16,128]{2,1,0:T(8,128)(2,1)} custom-call(f32[8,4,8,128]{3,2,1,0:T(8,128)S(1)} %bitcast.11, bf16[8,16,128]{2,1,0:T(8,128)(2,1)S(1)} %get-tuple-element.8.r_rows), custom_call_target="tpu_custom_call" | custom-call | tf_op jit(solution)/shard_map/home/pallas_call | solution.py:386

commit v10 on v9

--- a/solution.py
+++ b/solution.py
@@ -171,8 +171,9 @@
         out[:, at, :] = (r_rows[:, at, :].astype(f32) * total[w]).astype(bf16)
 
 
-BIG = 2.0**15
 EXACT = 256.0
+SHIFT = 4096.0
+ROUND = 1.5 * 2.0**23 * SHIFT
 
 
 def join_kernel(n_c, cap, split_w, srcs, tiles, held, out, s_ref, t_ref, own_ref, all_ref):
@@ -223,9 +224,7 @@
         for k, ref in enumerate((s_ref, t_ref)):
             first, c = stack(i, 2 * k, own), stack(i, 2 * k + 1, own)
             counts.append(mm_nt(c, first))
-            for w in own:
-                at = slice(w * KEYS, (w + 1) * KEYS)
-                ref[w, pl.ds(i * m, m), :] = jnp.concatenate([c[at], first[at]], 0).T
+            ref[pl.ds(i * m, m), :] = jnp.concatenate([c, first], 0).T
         return counts
 
     def all_counts(i):
@@ -237,8 +236,8 @@
         for count in own_found:
             same = iota(count.shape, 0) // KEYS == iota(count.shape, 1) // KEYS
             count = jnp.where(same, count, 0.0)
-            high = jnp.floor(count / EXACT) * EXACT
-            found.append((count - high, high))
+            high = jnp.floor(count / EXACT)
+            found.append((count - EXACT * high, high))
         more = jnp.maximum(jnp.max(found[0][1]), jnp.max(found[1][1])) > 0.0
         return [(low.astype(bf16), high.astype(bf16)) for low, high in found], more
 
@@ -264,15 +263,18 @@
         ra, rb = [jnp.concatenate([one_hot(rows, k)] * split_w, 0) for k in (4, 5)]
         (s_low, s_high), (t_low, t_high) = found
 
-        def sides(table, hot, kind_flag):
-            value = mm(table, hot).astype(bf16)
-            flag = jnp.where(hot_of(rows, kind_flag), jnp.zeros_like(key), jnp.full_like(key, -BIG))
-            return [jnp.concatenate([value[w * KEYS : (w + 1) * KEYS], flag], 0) for w in own]
-
-        def one(of_s, of_t, between, j, acc):
+        def side(table, hot, kind_flag):
+            value = mm(table, hot)
+            flag = lambda w: jnp.where(
+                hot_of(rows, kind_flag), jnp.zeros_like(key), jnp.full_like(key, -2 * EXACT * SHIFT**w)
+            )
+            value = [(value[w * KEYS : (w + 1) * KEYS] * SHIFT**w).astype(bf16) for w in own]
+            return jnp.concatenate(value + [flag(w) for w in own], 0)
+
+        def one(of_s, of_t, between, j, accs):
             at = pl.ds(j * m, m)
             rows = block_of(j)
-            xs, matches = [], []
+            xs, matches = [], [[] for _ in own]
             for left, ref, start in ((of_s, s_ref, 0), (of_t, t_ref, cap)):
                 x = rows[:, start // TILE : (start + cap) // TILE]
                 x = x.reshape(srcs // n_c, n_c, cap, LANES)
@@ -281,19 +283,33 @@
                     shifted = jnp.concatenate([x[:, n_c - w :], x[:, : n_c - w]], 1).reshape(m, LANES)
                     turned = jnp.concatenate([turned[:, : w * rows_of], shifted[:, w * rows_of :]], 1)
                 xs.append(turned.T)
+                if len(xs) in between:
+                    between[len(xs)]()
+                both = mm(ref[at], left)
+                if split_w == 2:
+                    second = (both + ROUND) - ROUND
+                    both = (both - second, second)
+                else:
+                    both = (both,)
                 for w in own:
-                    if len(matches) in between:
-                        between[len(matches)]()
-                    matches.append(jnp.maximum(mm(ref[w, at], left[w]), 0.0).astype(bf16))
-            xs = [x[w * rows_of : (w + 1) * rows_of] for x in xs for w in own]
-            return acc + mm(jnp.concatenate(xs, 1), jnp.concatenate(matches, 0))
-
-        def over(of_s, of_t, acc, between=()):
+                    matches[w].append(jnp.maximum(both[w].astype(bf16), jnp.zeros((), bf16)))
+            return tuple(
+                acc
+                + mm(
+                    jnp.concatenate([x[w * rows_of : (w + 1) * rows_of] for x in xs], 1),
+                    jnp.concatenate(matches[w], 0),
+                )
+                for w, acc in enumerate(accs)
+            )
+
+        def over(of_s, of_t, between=()):
             step = functools.partial(one, of_s, of_t, between)
-            return step(0, acc) if blocks == 1 else lax.fori_loop(0, blocks, step, acc)
-
-        acc = over(sides(t_low, ra, 5), sides(s_low, rb, 4), jnp.zeros((rows_of, m), f32), between)
-        again = lambda x: over(sides(t_high, ra, 5), sides(s_high, rb, 4), x)
+            accs = tuple(jnp.zeros((rows_of, m), f32) for _ in own)
+            accs = step(0, accs) if blocks == 1 else lax.fori_loop(0, blocks, step, accs)
+            return sum(acc * SHIFT**-w for w, acc in enumerate(accs))
+
+        acc = over(side(t_low, ra, 5), side(s_low, rb, 4), between)
+        again = lambda x: x + EXACT * over(side(t_high, ra, 5), side(s_high, rb, 4))
         return acc, lambda x: lax.cond(more, again, lambda x: x, x)
 
     def factor(i, table):
@@ -316,8 +332,8 @@
         found = tables(own_counts(0))
         halves = halves_of(all_counts(0))
         between = {
-            0: lambda: kept.update(table=scales(halves)),
-            split_w: lambda: kept.update(by=factor(0, kept["table"])),
+            1: lambda: kept.update(table=scales(halves)),
+            2: lambda: kept.update(by=factor(0, kept["table"])),
         }
         acc, rest = joins(0, *found, between)
         finish(0, rest(acc), kept["by"])
@@ -351,7 +367,7 @@
     total_slots = n * cap
     split_w = 2 if n_c % 2 == 0 and width == LANES and cap % 16 == 0 else 1
     meta_rows = 8 if n_c * cap == LANES else 4
-    assert n_c * cap in (LANES, LANES // 2) and n % (2 * n_c) == 0 and n * cap < BIG
+    assert n_c * cap in (LANES, LANES // 2) and n % (2 * n_c) == 0 and n * cap < EXACT**2
     tiles = (2 * cap + meta_rows) // TILE
     row = lambda x: x.reshape(1, x.shape[0])
     far = lambda x: pltpu.with_memory_space_constraint(x, pltpu.HBM)
@@ -374,7 +390,7 @@
     shares = pl.pallas_call(
         functools.partial(join_kernel, n_c, cap, split_w, srcs, tiles),
         out_shape=pltpu.VMEM((n, cap // split_w, width), f32),
-        scratch_shapes=[pltpu.VMEM((split_w, total_slots, LANES), bf16)] * 2
+        scratch_shapes=[pltpu.VMEM((total_slots, 2 * split_w * KEYS), bf16)] * 2
         + [
             pltpu.VMEM((2, split_w * KEYS, split_w * KEYS), f32),
             pltpu.VMEM((2, n_c * KEYS, n_c * KEYS), f32),

time: 32.9 us -> 32.7 us (level)
  no operation moved by 1% of the time
where the time goes in v10:
time: 32.7 us; the launch traced here: 32.5 us
  blocking collectives  28.9 us (88%)
  Pallas kernels  3.63 us (11%)
    all_to_all x1, blocking collectives, body(): held = lax.all_to_all(packed, AXES, split_axis=0, concat_axis=0, tiled=True)  17.8 us
    all_to_all x1, blocking collectives, body(): back = lax.all_to_all(shares, AXES, split_axis=0, concat_axis=0, tiled=True)  11.1 us
    pallas_call x1, Pallas kernels, body(): pl.pallas_call(functools.partial(join_kernel, n_c, cap, split_w, srcs, ti...  1.62 us
    pallas_call x1, Pallas kernels, body(): pl.pallas_call(functools.partial(pack_kernel, n_a, n_b, n_c, cap, split_w...  1.3 us
    pallas_call x1, Pallas kernels, body(): pl.pallas_call(functools.partial(home_kernel, split_w), out_shape=jax.Sha...  0.7 us

profile of v10, /device:TPU:0, one launch (start us, length us, event | category | flops | bytes accessed | tf_op | source)
XLA Modules:
  0.0 32.5 jit_solution(3676592845945515139)
XLA Ops:
  0.0 1.3 %pack.1 = (bf16[288,4,128]{2,1,0:T(4,128)(2,1)S(1)}, bf16[8,16,128]{2,1,0:T(8,128)(2,1)S(1)}) custom-call(bf16[16,16,128]{2,1,0:T(8,128)(2,1)} %bitcast.12, bf16[8,16,128]{2,1,0:T(8,128)(2,1)} %bitcast.13, bf16[8,16,128]{2,1,0:T(8,128)(2,1)} %bitcast.14, s32[1,256]{1,0:T(1,128)} %bitcast.15, s32[1,128]{1,0:T(1,128)} %bitcast.16, s32[1,128]{1,0:T(1,128)} %bitcast.17, ...), custom_call_target="tpu_custom_call" | custom-call | tf_op jit(solution)/shard_map/pack/pallas_call | solution.py:380
  1.3 17.8 %all_to_all.10.held = bf16[288,4,128]{2,1,0:T(4,128)(2,1)S(1)} all-to-all(bf16[288,4,128]{2,1,0:T(4,128)(2,1)S(1)} %get-tuple-element.7), channel_id=1, replica_groups=mesh['aa'=2,'ba'=4,'col'=4] {'aa','ba','col'}, dimensions={0} | all-to-all | bytes 589824 | tf_op jit(solution)/shard_map/all_to_all | solution.py:389
  19.1 1.6 %join.1 = f32[32,8,128]{2,1,0:T(8,128)S(1)} custom-call(bf16[288,4,128]{2,1,0:T(4,128)(2,1)S(1)} %all_to_all.10.held), custom_call_target="tpu_custom_call" | custom-call | tf_op jit(solution)/shard_map/join/pallas_call | solution.py:390
  20.7 11.1 %all_to_all.11 = f32[32,8,128]{2,1,0:T(8,128)S(1)} all-to-all(f32[32,8,128]{2,1,0:T(8,128)S(1)} %join.1), channel_id=1, replica_groups=mesh['aa'=2,'ba'=4,'col'=4] {'aa','ba','col'}, dimensions={0} | all-to-all | bytes 262144 | tf_op jit(solution)/shard_map/all_to_all | solution.py:401
  31.8 0.7 %home.1 = bf16[8,16,128]{2,1,0:T(8,128)(2,1)} custom-call(f32[8,4,8,128]{3,2,1,0:T(8,128)S(1)} %bitcast.11, bf16[8,16,128]{2,1,0:T(8,128)(2,1)S(1)} %get-tuple-element.8.r_rows), custom_call_target="tpu_custom_call" | custom-call | tf_op jit(solution)/shard_map/home/pallas_call | solution.py:402

commit v11 on v10

--- a/solution.py
+++ b/solution.py
@@ -77,8 +77,10 @@
         spread = (iota((groups, slots), 1) // cap == iota((groups, slots), 0)).astype(bf16)
         cnt = jnp.broadcast_to(cnt_ref[...].astype(f32).astype(bf16), (8, groups))
         live = (iota((1, slots), 1) % cap).astype(f32) < mm(cnt, spread)[0:1]
-        first = jnp.where(live, lax.div(keys, KEYS).astype(f32), -1.0)
-        second = jnp.where(live, lax.rem(keys, KEYS).astype(f32), -1.0)
+        keys = keys.astype(f32)
+        high = jnp.floor(keys * (1.0 / KEYS))
+        first = jnp.where(live, high, -1.0)
+        second = jnp.where(live, keys - KEYS * high, -1.0)
         return first, second
 
     def at(vec, start):

time: 32.7 us -> 32.7 us (level)
  no operation moved by 1% of the time
where the time goes in v11:
time: 32.7 us; the launch traced here: 32.5 us
  blocking collectives  28.9 us (88%)
  Pallas kernels  3.63 us (11%)
    all_to_all x1, blocking collectives, body(): held = lax.all_to_all(packed, AXES, split_axis=0, concat_axis=0, tiled=True)  17.8 us
    all_to_all x1, blocking collectives, body(): back = lax.all_to_all(shares, AXES, split_axis=0, concat_axis=0, tiled=True)  11.1 us
    pallas_call x1, Pallas kernels, body(): pl.pallas_call(functools.partial(join_kernel, n_c, cap, split_w, srcs, ti...  1.62 us
    pallas_call x1, Pallas kernels, body(): pl.pallas_call(functools.partial(pack_kernel, n_a, n_b, n_c, cap, split_w...  1.3 us
    pallas_call x1, Pallas kernels, body(): pl.pallas_call(functools.partial(home_kernel, split_w), out_shape=jax.Sha...  0.7 us

profile of v11, /device:TPU:0, one launch (start us, length us, event | category | flops | bytes accessed | tf_op | source)
XLA Modules:
  0.0 32.5 jit_solution(2947104252995394725)
XLA Ops:
  0.0 1.3 %pack.1 = (bf16[288,4,128]{2,1,0:T(4,128)(2,1)S(1)}, bf16[8,16,128]{2,1,0:T(8,128)(2,1)S(1)}) custom-call(bf16[16,16,128]{2,1,0:T(8,128)(2,1)} %bitcast.12, bf16[8,16,128]{2,1,0:T(8,128)(2,1)} %bitcast.13, bf16[8,16,128]{2,1,0:T(8,128)(2,1)} %bitcast.14, s32[1,256]{1,0:T(1,128)} %bitcast.15, s32[1,128]{1,0:T(1,128)} %bitcast.16, s32[1,128]{1,0:T(1,128)} %bitcast.17, ...), custom_call_target="tpu_custom_call" | custom-call | tf_op jit(solution)/shard_map/pack/pallas_call | solution.py:382
  1.3 17.8 %all_to_all.10.held = bf16[288,4,128]{2,1,0:T(4,128)(2,1)S(1)} all-to-all(bf16[288,4,128]{2,1,0:T(4,128)(2,1)S(1)} %get-tuple-element.7), channel_id=1, replica_groups=mesh['aa'=2,'ba'=4,'col'=4] {'aa','ba','col'}, dimensions={0} | all-to-all | bytes 589824 | tf_op jit(solution)/shard_map/all_to_all | solution.py:391
  19.1 1.6 %join.1 = f32[32,8,128]{2,1,0:T(8,128)S(1)} custom-call(bf16[288,4,128]{2,1,0:T(4,128)(2,1)S(1)} %all_to_all.10.held), custom_call_target="tpu_custom_call" | custom-call | tf_op jit(solution)/shard_map/join/pallas_call | solution.py:392
  20.7 11.1 %all_to_all.11 = f32[32,8,128]{2,1,0:T(8,128)S(1)} all-to-all(f32[32,8,128]{2,1,0:T(8,128)S(1)} %join.1), channel_id=1, replica_groups=mesh['aa'=2,'ba'=4,'col'=4] {'aa','ba','col'}, dimensions={0} | all-to-all | bytes 262144 | tf_op jit(solution)/shard_map/all_to_all | solution.py:403
  31.8 0.7 %home.1 = bf16[8,16,128]{2,1,0:T(8,128)(2,1)} custom-call(f32[8,4,8,128]{3,2,1,0:T(8,128)S(1)} %bitcast.11, bf16[8,16,128]{2,1,0:T(8,128)(2,1)S(1)} %get-tuple-element.8.r_rows), custom_call_target="tpu_custom_call" | custom-call | tf_op jit(solution)/shard_map/home/pallas_call | solution.py:404
